TPU v7x, 128 devices: a whole 4x4x4 slice. The times are simulated.
128 devices in a mesh: space: 32 (over x_lo, z, y), tm: 4 (over x_hi, core).
Axes of the slice: x: 4 (x_hi: 2, x_lo: 2; x = x_hi * 2 + x_lo), y: 4, z: 4, core: 2. Of those that a mesh axis runs over, the one named last changes fastest.
Arguments:
- innovations: bfloat16 [12, 32, 768, 1536], P('tm', None, 'space'), may hold values from -6 to 6
- obs_counts: int32 [12, 192, 384], P('tm', 'space'), may hold values from 0 to 3
- diffusion: float32 [32, 192, 384], P(None, 'space'), may hold values from 0.01 to 0.1
- courant: float32 [32, 192, 384], P(None, 'space'), may hold values from 0 to 0.4
Outputs:
- increment: float32 [32, 768, 1536], P('tm', 'space')
- residual: float32 [32, 192, 384], P('tm', 'space')
All inputs are finite; a program needn't handle non-finite values.
Results may differ from a plain program's by a relative error of at most 0.0003.
Values sent between devices are 32-bit elements; how exact they have to be, the bound alone decides.
No kernel may reach another device: no remote copies, remote signals or barrier semaphores. Data moves between devices by JAX's collectives and lax.ppermute only.
A program may use at most 192 MiB of HBM per device.

v0:
```python
import functools

import jax
import jax.numpy as jnp
from jax import lax
from jax.sharding import Mesh
from jax.sharding import PartitionSpec as P

ITERS = 3
SPACE = ("space_0", "space_1", "space_2")
SPACE_TM = ("space_0", "space_1", "space_2", "tm_0", "tm_1")
TM = ("tm_0", "tm_1")


def padded_2(cells, sides, width):
    for axis, dim in sides:
        count = lax.axis_size(axis)
        ends = count - 1
        head = lax.slice_in_dim(cells, 0, width, axis=dim)
        tail = lax.slice_in_dim(cells, cells.shape[dim] - width, cells.shape[dim], axis=dim)
        cells = jnp.concatenate(
            [
                lax.ppermute(tail, axis, [(i, (i + 1) % count) for i in range(ends)]),
                cells,
                lax.ppermute(head, axis, [((i + 1) % count, i) for i in range(ends)]),
            ],
            axis=dim,
        )
    return cells


def one_axis_at_a_time(x, axes):
    return functools.reduce(lax.psum, axes, x)


def in_blocks(x, dim, count):
    lengths = x.shape
    tiles = x.reshape(*lengths[:dim], count, lengths[dim] // count, *lengths[dim + 1 :])
    return jnp.moveaxis(tiles, dim, 0)


def joined_along(tiles, dim):
    tiles = jnp.moveaxis(tiles, 0, dim)
    lengths = tiles.shape
    return tiles.reshape(*lengths[:dim], lengths[dim] * lengths[dim + 1], *lengths[dim + 2 :])


def turned_blocks(tiles, axes, sequence):
    inside = tiles.shape[1:]
    out = tiles.reshape(*(lax.axis_size(a) for a in axes), *inside)
    for k in sequence:
        out = lax.all_to_all(out, axes[k], k, k, tiled=True)
    return out.reshape(-1, *inside)


def exchange_by_chip(x, groups, sequence, split_dim, concat_dim):
    count = lax.axis_size(groups[0]) * lax.axis_size(groups[1])
    tiles = in_blocks(x, split_dim, count)
    return joined_along(turned_blocks(tiles, groups, sequence), concat_dim)


def laplace_rows(padded, state_field):
    return (
        padded[:, 2:, :]
        + padded[:, :-2, :]
        + jnp.roll(state_field, 1, 2)
        + jnp.roll(state_field, -1, 2)
        - 4.0 * state_field
    )


def tangent(state_field, diffusion, courant):
    padded = padded_2(state_field, ((SPACE, 1),), 1)
    return (
        state_field
        + diffusion * laplace_rows(padded, state_field)
        - courant * (state_field - jnp.roll(state_field, 1, 2))
    )


def adjoint(state_field, diffusion, courant):
    carried = courant * state_field
    spread = diffusion * state_field
    padded = padded_2(spread, ((SPACE, 1),), 1)
    return state_field + laplace_rows(padded, spread) - carried + jnp.roll(carried, -1, 2)


def level_squares(residual):
    return one_axis_at_a_time(jnp.sum(residual * residual), SPACE_TM)


def level_curve(direction, hessian_image):
    return one_axis_at_a_time(jnp.sum(direction * hessian_image), SPACE_TM)


def solve_inner(rhs_field, hessian_part, norm_fn, curve_fn):
    control = jnp.zeros_like(rhs_field)
    residual = rhs_field
    direction = rhs_field
    norm_now = norm_fn(residual)
    for iter_no in range(ITERS):
        hessian_image = direction + hessian_part(direction)
        step_len = norm_now / curve_fn(direction, hessian_image)
        control = control + step_len * direction
        residual = residual - step_len * hessian_image
        if iter_no + 1 < ITERS:
            norm_next = norm_fn(residual)
            direction = residual + norm_next / norm_now * direction
            norm_now = norm_next
    return (control, residual)


def on_device(innovations, obs_counts, diffusion, courant):
    step_dev = obs_counts.shape[0]
    n_sections = lax.axis_size(TM)
    section_pos = lax.axis_index(TM)
    total_steps = step_dev * n_sections
    weights = obs_counts.astype(jnp.float32)[:, None]
    levels, fine_rows, fine_cols = (
        innovations.shape[1],
        innovations.shape[2],
        innovations.shape[3],
    )
    lev_part = levels // n_sections
    blocks = innovations.reshape(step_dev, levels, fine_rows // 4, 4, fine_cols // 4, 4).astype(
        jnp.float32
    )
    forcing = weights * jnp.mean(blocks, axis=(3, 5))
    all_weights = lax.all_gather(obs_counts, TM, axis=0, tiled=True).astype(jnp.float32)[:, None]
    all_forcing = exchange_by_chip(forcing, ("tm_0", "tm_1"), (1, 0), 1, 0)
    diff_part = lax.dynamic_slice_in_dim(diffusion, section_pos * lev_part, lev_part, 0)
    cour_part = lax.dynamic_slice_in_dim(courant, section_pos * lev_part, lev_part, 0)

    def level_back(terms):
        current = terms[total_steps - 1]
        for step_no in range(total_steps - 2, -1, -1):
            current = terms[step_no] + adjoint(current, diff_part, cour_part)
        return current

    def level_hess(state_field):
        records = []
        for step_no in range(total_steps):
            records.append(all_weights[step_no] * state_field)
            if step_no + 1 < total_steps:
                state_field = tangent(state_field, diff_part, cour_part)
        return level_back(jnp.stack(records))

    control, residual = solve_inner(level_back(all_forcing), level_hess, level_squares, level_curve)
    increment = jnp.repeat(jnp.repeat(control, 4, axis=1), 4, axis=2)
    return (increment, residual)


def solution(mesh):
    torus = Mesh(
        mesh.devices.reshape(2, 4, 4, 2, 2), ("space_0", "space_1", "space_2", "tm_0", "tm_1")
    )
    return jax.shard_map(
        on_device,
        mesh=torus,
        in_specs=(
            P(TM, None, SPACE, None),
            P(TM, SPACE, None),
            P(None, SPACE, None),
            P(None, SPACE, None),
        ),
        out_specs=(P(TM, SPACE, None), P(TM, SPACE, None)),
        check_vma=False,
    )
```

profile of v0, /device:TPU:1, one launch (start us, length us, event | category | flops | bytes accessed | tf_op | source)
XLA Modules:
  0.0 1253.6 jit_solution(14958787552105750549)
XLA Ops:
  0.6 30.1 %copy.21 = f32[3,32,24,1536]{1,3,2,0:T(8,128)} copy(bf16[3,32,24,1536]{3,2,1,0:T(8,128)(2,1)} %param.4) | data formatting | bytes 21233664 | tf_op jit(solution)/shard_map/convert_element_type | solution.py:125
  30.8 40.6 %reduce_sum.65 = f32[3,32,6,384]{1,3,2,0:T(8,128)} reduce(f32[3,32,6,4,384,4]{1,5,4,3,2,0:T(4,128)} %bitcast.96, f32[]{:T(128)} %constant.8.clone.1), dimensions={3,5}, to_apply=%region_0.0 | reduce | flops 3317760 | bytes 15040516 | tf_op jit(solution)/shard_map/reduce_sum | solution.py:128
  84.6 15.8 %all_gather.3 = s32[12,6,384]{2,1,0:T(8,128)S(1)} all-gather(s32[3,6,384]{2,1,0:T(8,128)S(1)} %copy-done.3), channel_id=1, replica_groups=mesh['space_0'=2,'space_1'=4,'space_2'=4,'tm_0'=2,'tm_1'=2] {'tm_0','tm_1'}, dimensions={0}, use_global_device_ids=true | all-gather | bytes 138240 | tf_op jit(solution)/shard_map/all_gather | solution.py:129
  134.9 6.4 collective-permute-start.9
  145.4 6.4 collective-permute-start.11
  155.9 6.4 collective-permute-start.13
  166.4 6.4 collective-permute-start.15
  176.9 6.4 collective-permute-start.17
  187.5 6.4 collective-permute-start.19
  198.0 6.4 collective-permute-start.21
  207.5 6.4 collective-permute-start.23
  217.1 6.4 collective-permute-start.25
  226.7 6.4 collective-permute-start.27
  236.3 6.4 collective-permute-start.29
  245.9 6.4 collective-permute-start.31
  255.5 6.4 collective-permute-start.33
  265.1 6.4 collective-permute-start.35
  274.7 6.4 collective-permute-start.37
  284.3 6.4 collective-permute-start.39
  293.9 6.4 collective-permute-start.41
  303.5 6.4 collective-permute-start.43
  312.2 6.7 collective-permute-start.45
  321.2 6.4 collective-permute-start.47
  329.9 6.4 collective-permute-start.49
  338.6 6.4 collective-permute-start.51
  347.4 6.4 collective-permute-start.53
  356.1 6.4 collective-permute-start.55
  364.8 6.4 collective-permute-start.57
  373.5 6.4 collective-permute-start.59
  382.3 8.2 collective-permute-start.61
  393.0 8.5 collective-permute-start.63
  403.8 8.5 collective-permute-start.65
  413.8 81.6 %all-reduce.4 = (f32[]{:T(128)}, f32[]{:T(128)}) all-reduce(f32[]{:T(128)} %get-tuple-element.11, f32[]{:T(128)} %get-tuple-element.10), channel_id=1, replica_groups=mesh['space_0'=2,'space_1'=4,'space_2'=4,'tm_0'=2,'tm_1'=2] {'space_0'}, use_global_device_ids=true, to_apply=%region_2.3 | all-reduce | flops 2 | bytes 16 | tf_op jit(solution)/shard_map/psum | solution.py:33
  495.4 6.6 all-reduce.1
  502.0 7.2 all-reduce
  515.1 46.9 %all-reduce.2 = (f32[]{:T(128)}, f32[]{:T(128)}) all-reduce(f32[]{:T(128)} %get-tuple-element.18, f32[]{:T(128)} %get-tuple-element.19), channel_id=1, replica_groups=mesh['space_0'=2,'space_1'=4,'space_2'=4,'tm_0'=2,'tm_1'=2] {'tm_1'}, use_global_device_ids=true, to_apply=%region_6.7 | all-reduce | flops 2 | bytes 16 | tf_op jit(solution)/shard_map/psum | solution.py:33
  568.4 7.8 psum.221
  576.2 8.2 psum.222
  590.4 9.1 psum.224
  648.7 6.4 collective-permute-start.79
  658.3 6.4 collective-permute-start.81
  667.9 6.4 collective-permute-start.83
  677.5 6.4 collective-permute-start.85
  687.1 6.4 collective-permute-start.87
  695.8 6.4 collective-permute-start.89
  704.5 6.4 collective-permute-start.91
  713.2 6.4 collective-permute-start.93
  721.9 6.4 collective-permute-start.95
  730.6 6.4 collective-permute-start.97
  774.2 6.4 collective-permute-start.107
  790.8 62.3 %psum.225 = f32[]{:T(128)} all-reduce(f32[]{:T(128)} %get-tuple-element.48), channel_id=1, replica_groups=mesh['space_0'=2,'space_1'=4,'space_2'=4,'tm_0'=2,'tm_1'=2] {'space_0'}, use_global_device_ids=true, to_apply=%region_20.21 | all-reduce | flops 1 | bytes 8 | tf_op jit(solution)/shard_map/psum | solution.py:33
  853.2 6.6 psum.226
  859.8 7.2 psum.227
  872.9 34.0 %psum.229 = f32[]{:T(128)} all-reduce(f32[]{:T(128)} %psum.228), channel_id=1, replica_groups=mesh['space_0'=2,'space_1'=4,'space_2'=4,'tm_0'=2,'tm_1'=2] {'tm_1'}, use_global_device_ids=true, to_apply=%region_24.25 | all-reduce | flops 1 | bytes 8 | tf_op jit(solution)/shard_map/psum | solution.py:33
  913.2 7.8 psum.231
  921.1 8.2 psum.232
  935.2 9.1 psum.234
  1057.6 6.6 collective-permute-start.139
  1109.8 6.4 collective-permute-start.151
  1118.6 6.4 collective-permute-start.153
  1126.5 62.3 %psum.235 = f32[]{:T(128)} all-reduce(f32[]{:T(128)} %get-tuple-element.22), channel_id=1, replica_groups=mesh['space_0'=2,'space_1'=4,'space_2'=4,'tm_0'=2,'tm_1'=2] {'space_0'}, use_global_device_ids=true, to_apply=%region_32.33 | all-reduce | flops 1 | bytes 8 | tf_op jit(solution)/shard_map/psum | solution.py:33
  1188.8 6.6 psum.236
  1195.4 7.2 psum.237
  1208.5 34.0 %psum.239 = f32[]{:T(128)} all-reduce(f32[]{:T(128)} %psum.238), channel_id=1, replica_groups=mesh['space_0'=2,'space_1'=4,'space_2'=4,'tm_0'=2,'tm_1'=2] {'tm_1'}, use_global_device_ids=true, to_apply=%region_36.37 | all-reduce | flops 1 | bytes 8 | tf_op jit(solution)/shard_map/psum | solution.py:33
  (740 shorter events, 463.1 us)
Async XLA Ops:
  80.5 19.9 %all-to-all-start.1 = ((f32[2,2,3,8,6,384]{5,3,1,4,2,0:T(8,128)}), f32[2,2,3,8,6,384]{5,3,1,4,2,0:T(8,128)S(1)}, u32[]{:S(2)}, u32[]{:S(2)}) async-start(f32[2,2,3,8,6,384]{5,3,1,4,2,0:T(8,128)} %copy.24), calls=%async_computation.1 | async-start | bytes 1769472 | tf_op jit(solution)/shard_map/all_to_all | solution.py:52
  133.6 7.8 collective-permute-start.8
  144.1 7.8 collective-permute-start.10
  154.6 7.8 collective-permute-start.12
  165.1 7.8 collective-permute-start.14
  175.6 7.8 collective-permute-start.16
  186.2 7.8 collective-permute-start.18
  196.7 7.8 collective-permute-start.20
  206.2 7.7 collective-permute-start.22
  215.8 7.7 collective-permute-start.24
  225.4 7.7 collective-permute-start.26
  235.0 7.7 collective-permute-start.28
  244.6 7.7 collective-permute-start.30
  254.2 7.7 collective-permute-start.32
  263.8 7.7 collective-permute-start.34
  273.4 7.7 collective-permute-start.36
  283.0 7.7 collective-permute-start.38
  292.6 7.7 collective-permute-start.40
  302.2 7.7 collective-permute-start.42
  310.9 8.2 collective-permute-start.44
  319.9 7.8 collective-permute-start.46
  328.6 7.8 collective-permute-start.48
  337.3 7.8 collective-permute-start.50
  346.1 7.8 collective-permute-start.52
  354.8 7.8 collective-permute-start.54
  363.5 7.8 collective-permute-start.56
  372.2 7.9 collective-permute-start.58
  381.0 9.7 collective-permute-start.60
  382.3 9.0 collective-permute-start.61
  391.5 10.1 collective-permute-start.62
  393.0 9.3 collective-permute-start.63
  402.5 9.9 collective-permute-start.64
  403.8 9.3 collective-permute-start.65
  647.4 7.7 collective-permute-start.78
  657.0 7.7 collective-permute-start.80
  666.6 7.7 collective-permute-start.82
  676.2 7.7 collective-permute-start.84
  685.8 7.7 collective-permute-start.86
  694.5 7.8 collective-permute-start.88
  703.2 7.8 collective-permute-start.90
  711.9 7.8 collective-permute-start.92
  720.6 7.8 collective-permute-start.94
  729.3 7.8 collective-permute-start.96
  738.0 7.8 collective-permute-start.98
  746.8 7.8 collective-permute-start.100
  755.5 7.8 collective-permute-start.102
  764.2 7.8 collective-permute-start.104
  772.9 7.9 collective-permute-start.106
  781.7 7.8 collective-permute-start.108
  986.7 7.7 collective-permute-start.122
  995.4 7.7 collective-permute-start.124
  1004.1 7.7 collective-permute-start.126
  1012.7 7.7 collective-permute-start.128
  1030.1 7.8 collective-permute-start.132
  1038.8 7.8 collective-permute-start.134
  1047.6 7.8 collective-permute-start.136
  1056.3 8.1 collective-permute-start.138
  1065.0 7.8 collective-permute-start.140
  1073.7 7.8 collective-permute-start.142
  1082.4 7.8 collective-permute-start.144
  1091.1 7.8 collective-permute-start.146
  1099.8 7.8 collective-permute-start.148
  1108.5 7.9 collective-permute-start.150
  1117.3 7.8 collective-permute-start.152
  (95 other events, 712.9 us)
where the time goes:
time: 1260 us; the launch traced here: 1250 us
  starting transfers between devices  570 us (45%)
  blocking collectives  472 us (37%)
  other arithmetic  89.7 us (7%)
  local copies, waits for them, and re-layouts  58.6 us (5%)
  waiting for transfers between devices  52.2 us (4%)
    ppermute x77, starting transfers between devices, padded_2(): lax.ppermute(tail, axis, [(i, (i + 1) % count) for i in range(ends)])  466 us
    psum x25, blocking collectives, one_axis_at_a_time(): return functools.reduce(lax.psum, axes, x)  451 us
    ppermute x77, starting transfers between devices, padded_2(): lax.ppermute(head, axis, [((i + 1) % count, i) for i in range(ends)])  99.7 us
    ppermute x77, waiting for transfers between devices, padded_2(): lax.ppermute(tail, axis, [(i, (i + 1) % count) for i in range(ends)])  52 us
    reduce_sum x1, other arithmetic, on_device(): forcing = weights * jnp.mean(blocks, axis=(3, 5))  40.6 us
    convert_element_type x1, local copies, waits for them, and re-layouts, on_device(): innovations.reshape(step_dev, levels, fine_rows // 4, 4, fine_cols // 4, 4)  30.1 us
  transfers between devices with their start and end apart: 155, of which 77 were waited for; matrix products, arithmetic and copies ran while one was open for 1% of the time, Pallas kernels for 0%

commit v1 on v0

v1 whole, which is shorter than its diff:
```python
import functools

import jax
import jax.numpy as jnp
import numpy as np
from jax import lax
from jax.experimental import pallas as pl
from jax.experimental.pallas import tpu as pltpu
from jax.sharding import Mesh
from jax.sharding import PartitionSpec as P

SPACE = ("space_0", "space_1", "space_2")
TM = ("tm_0", "tm_1")
SWAP = [(0, 1), (1, 0)]
F32 = jnp.float32
BF16 = jnp.bfloat16

NI, NJ = 24, 3
REGS = NI * NJ
ROWS = REGS * 8
STEPS = 12
ITERS = 3
VMEM = pl.BlockSpec(memory_space=pltpu.VMEM)
SMEM = pl.BlockSpec(memory_space=pltpu.SMEM)


def column_order():
    return (np.arange(128)[None, :] * NJ + np.arange(NJ)[:, None]).reshape(-1)


def matrices():
    order = column_order()
    pick = np.zeros((384, 384), np.float32)
    pick[order, np.arange(384)] = 1.0
    mean = np.repeat(pick, 4, axis=0) / 16.0
    spread = np.repeat(pick, 4, axis=0).T
    return (
        jnp.asarray(pick, BF16),
        jnp.asarray(mean, BF16),
        jnp.asarray(spread, BF16),
        jnp.asarray(pick.T, BF16),
    )


def exact_dot(x, one_hot):
    a = x.astype(BF16)
    rest = x - a.astype(F32)
    b = rest.astype(BF16)
    c = (rest - b.astype(F32)).astype(BF16)
    n = x.shape[0]
    y = jnp.dot(jnp.concatenate([a, b, c], 0), one_hot, preferred_element_type=F32)
    return y[:n] + y[n : 2 * n] + y[2 * n :]


def prepare_kernel(core_ref, counts_ref, diff_ref, cour_ref, pick_ref, out_ref, wt_ref, rows_ref):
    levels = diff_ref.shape[0]

    @pl.when(core_ref[0] == 0)
    def _():
        for k in range(levels):
            rows_ref[pl.ds(6 * k, 6), :] = diff_ref[k]

    @pl.when(core_ref[0] != 0)
    def _():
        for k in range(levels):
            rows_ref[pl.ds(6 * k, 6), :] = cour_ref[k]

    field = exact_dot(rows_ref[...], pick_ref[...])
    for k in range(levels):
        for j in range(NJ):
            out_ref[k, pl.ds(6 * j, 6), :] = field[6 * k : 6 * k + 6, 128 * j : 128 * j + 128]
    for t in range(3):
        w = jnp.dot(
            counts_ref[t].astype(F32).astype(BF16), pick_ref[...], preferred_element_type=F32
        )
        for k in range(8):
            wt_ref[t, pl.ds(6 * k, 6), :] = w
        for j in range(NJ):
            piece = w[:, 128 * j : 128 * j + 128]
            for k in range(levels):
                out_ref[k, pl.ds(18 + 18 * t + 6 * j, 6), :] = piece


def prepare(core, counts, diffusion, courant, pick):
    levels = diffusion.shape[0]
    return pl.pallas_call(
        prepare_kernel,
        name="prepare",
        out_shape=(
            jax.ShapeDtypeStruct((levels, 72, 128), F32),
            jax.ShapeDtypeStruct((3, 48, 384), F32),
        ),
        in_specs=[SMEM, VMEM, VMEM, VMEM, VMEM],
        out_specs=(VMEM, VMEM),
        scratch_shapes=[pltpu.VMEM((levels * 6, 384), F32)],
        cost_estimate=pl.CostEstimate(flops=10**9, bytes_accessed=3 * 10**6, transcendentals=0),
    )(core, counts, diffusion, courant, pick)


def restrict_kernel(fine_ref, wt_ref, mean_ref, out_ref, sums_ref):
    for t in range(3):
        sums = jnp.dot(fine_ref[t], mean_ref[...], preferred_element_type=F32)
        for j in range(NJ):
            sums_ref[3 * t + j] = sums[:, 128 * j : 128 * j + 128]
        for j in range(NJ):
            z = (
                sums_ref[3 * t + j, pl.ds(0, 48, stride=4), :]
                + sums_ref[3 * t + j, pl.ds(1, 48, stride=4), :]
                + sums_ref[3 * t + j, pl.ds(2, 48, stride=4), :]
                + sums_ref[3 * t + j, pl.ds(3, 48, stride=4), :]
            ) * wt_ref[t, :, 128 * j : 128 * j + 128]
            for k in range(8):
                out_ref[k, pl.ds(18 * t + 6 * j, 6), :] = z[6 * k : 6 * k + 6]


def restrict(fine, wt, mean):
    return pl.pallas_call(
        restrict_kernel,
        name="restrict",
        grid=(4,),
        out_shape=jax.ShapeDtypeStruct((32, 54, 128), F32),
        in_specs=[
            pl.BlockSpec((3, 192, 1536), lambda g: (0, g, 0)),
            pl.BlockSpec((3, 48, 384), lambda g: (0, 0, 0)),
            pl.BlockSpec((1536, 384), lambda g: (0, 0)),
        ],
        out_specs=pl.BlockSpec((8, 54, 128), lambda g: (g, 0, 0)),
        scratch_shapes=[pltpu.VMEM((9, 192, 128), F32)],
        cost_estimate=pl.CostEstimate(flops=3 * 10**9, bytes_accessed=9 * 10**6, transcendentals=0),
    )(fine, wt, mean)


def reg(ref, base, i, j):
    return ref[pl.ds((base + i * NJ + j) * 8, 8), :]


def put(ref, base, i, j, value):
    ref[pl.ds((base + i * NJ + j) * 8, 8), :] = value


def taken(ref, width, first, i, j):
    start = (i // 6) * width + first + 6 * j + i % 6
    return ref[pl.ds(start, 8, stride=4 * width), :]


def edges():
    sub = lax.broadcasted_iota(jnp.int32, (8, 128), 0)
    first, last = sub == 0, sub == 7
    north = lambda x: jnp.where(first, 0.0, pltpu.roll(x, 1, 0))
    south = lambda x: jnp.where(last, 0.0, pltpu.roll(x, 7, 0))
    return north, south


def west(row, j):
    return row[j - 1] if j else pltpu.roll(row[NJ - 1], 1, 1)


def east(row, j):
    return row[j + 1] if j + 1 < NJ else pltpu.roll(row[0], 127, 1)


def tangent_step(src, sb, dst, db, coef):
    north, south = edges()
    load = lambda i: [reg(src, sb, i, j) for j in range(NJ)]
    first, last = load(0), load(NI - 1)
    above = [north(x) for x in last]
    here = first
    for i in range(NI):
        below = load(i + 1) if i + 1 < NI else [south(x) for x in first]
        for j in range(NJ):
            put(
                dst,
                db,
                i,
                j,
                reg(coef, 0, i, j) * here[j]
                + reg(coef, REGS, i, j) * (above[j] + below[j] + east(here, j))
                + reg(coef, 2 * REGS, i, j) * west(here, j),
            )
        above, here = here, below


def adjoint_step(lam, coef, term):
    north, south = edges()

    def load(i):
        y = [reg(lam, 0, i, j) for j in range(NJ)]
        return y, [reg(coef, REGS, i, j) * y[j] for j in range(NJ)]

    above = [north(z) for z in load(NI - 1)[1]]
    y, here = load(0)
    wrap = [south(z) for z in here]
    for i in range(NI):
        y_next, below = load(i + 1) if i + 1 < NI else (None, wrap)
        both = [reg(coef, 2 * REGS, i, j) * y[j] for j in range(NJ)]
        new = [
            reg(coef, 0, i, j) * y[j] + (above[j] + below[j]) + (west(here, j) + east(both, j))
            for j in range(NJ)
        ]
        for j in range(NJ):
            add = term(i, j)
            put(lam, 0, i, j, new[j] if add is None else new[j] + add)
        above, here, y = here, below, y_next


def rhs_kernel(place_ref, own_ref, other_ref, f_ref, part_ref, coef_ref):
    core = place_ref[0]
    block = place_ref[1]

    def coefficients(diff_ref, cour_ref):
        for i in range(NI):
            for j in range(NJ):
                d = taken(diff_ref, 72, 0, i, j)
                c = taken(cour_ref, 72, 0, i, j)
                put(coef_ref, 0, i, j, 1.0 - 4.0 * d - c)
                put(coef_ref, REGS, i, j, d)
                put(coef_ref, 2 * REGS, i, j, d + c)

    @pl.when(core == 0)
    def _():
        coefficients(own_ref, other_ref)

    @pl.when(core != 0)
    def _():
        coefficients(other_ref, own_ref)

    for i in range(NI):
        for j in range(NJ):
            put(part_ref, 0, i, j, taken(f_ref, 54, 36, i, j))
    for t in (1, 0):
        adjoint_step(part_ref, coef_ref, lambda i, j: taken(f_ref, 54, 18 * t, i, j))

    def more(_, carry):
        adjoint_step(part_ref, coef_ref, lambda i, j: None)
        return carry

    lax.fori_loop(0, 3 * block, more, 0)


def rhs_part(place, own, other, f):
    return pl.pallas_call(
        rhs_kernel,
        name="rhs_part",
        out_shape=(
            jax.ShapeDtypeStruct((ROWS, 128), F32),
            jax.ShapeDtypeStruct((3 * ROWS, 128), F32),
        ),
        in_specs=[SMEM, VMEM, VMEM, VMEM],
        out_specs=(VMEM, VMEM),
        cost_estimate=pl.CostEstimate(flops=10**9, bytes_accessed=4 * 10**6, transcendentals=0),
    )(place, own.reshape(-1, 128), other.reshape(-1, 128), f.reshape(-1, 128))


def total(x):
    return jnp.sum(jnp.sum(x, axis=0, keepdims=True), axis=1, keepdims=True)


def ratio(a, b):
    return jnp.where(b > 0.0, a / jnp.where(b > 0.0, b, 1.0), 0.0)


def krylov_kernel(
    place_ref, p_ref, pc_ref, near_ref, far_ref, coef_ref, w0, w1, w2, w3, out_ref, v, xs, lam, wbuf
):
    core = place_ref[0]
    block = place_ref[1]
    for ref, flip in ((w0, 0), (w1, 1), (w2, 2), (w3, 3)):
        base = jnp.bitwise_xor(block, flip) * 3 * REGS
        for t in range(3):
            for i in range(NI):
                for j in range(NJ):
                    wbuf[pl.ds(pl.multiple_of((base + t * REGS + i * NJ + j) * 8, 8), 8), :] = taken(
                        ref, 72, 18 + 18 * t, i, j
                    )

    half = REGS // 2
    acc = jnp.zeros((8, 128), F32)

    def first(lo_ref, hi_ref):
        for r in range(REGS):
            far = lo_ref if r < half else hi_ref
            rows = pl.ds(r * 8, 8)
            v[rows, :] = (p_ref[rows, :] + pc_ref[rows, :]) + far[pl.ds((r % half) * 8, 8), :]

    @pl.when(core == 0)
    def _():
        first(near_ref, far_ref)

    @pl.when(core != 0)
    def _():
        first(far_ref, near_ref)

    for r in range(REGS):
        x = v[pl.ds(r * 8, 8), :]
        acc = acc + x * x

    lane = lax.broadcasted_iota(jnp.int32, (8, 128), 1)

    def product(k, carry):
        norm, before, table = carry
        base = pl.multiple_of(k * ROWS, 8)
        prev = pl.multiple_of(jnp.maximum(k - 1, 0) * ROWS, 8)
        for r in range(REGS):
            xs[pl.ds(r * 8, 8), :] = v[pl.ds(base + r * 8, 8), :]
        for t in range(STEPS - 1):
            tangent_step(xs, t * REGS, xs, (t + 1) * REGS, coef_ref)
        last = (STEPS - 1) * REGS
        for r in range(REGS):
            lam[pl.ds(r * 8, 8), :] = (
                wbuf[pl.ds((last + r) * 8, 8), :] * xs[pl.ds((last + r) * 8, 8), :]
            )
        for t in range(STEPS - 2, -1, -1):
            adjoint_step(
                lam,
                coef_ref,
                lambda i, j, t=t: reg(wbuf, t * REGS, i, j) * reg(xs, t * REGS, i, j),
            )
        dot = jnp.zeros((8, 128), F32)
        for r in range(REGS):
            x = xs[pl.ds(r * 8, 8), :]
            image = x + lam[pl.ds(r * 8, 8), :]
            lam[pl.ds(r * 8, 8), :] = image
            dot = dot + x * image
        a = ratio(total(dot), norm)
        b = jnp.where(k > 0, ratio(norm, before), 0.0)
        new = jnp.zeros((8, 128), F32)
        for r in range(REGS):
            x = (
                lam[pl.ds(r * 8, 8), :]
                - a * xs[pl.ds(r * 8, 8), :]
                - b * v[pl.ds(prev + r * 8, 8), :]
            )
            v[pl.ds(base + ROWS + r * 8, 8), :] = x
            new = new + x * x
        table = jnp.where(lane == k, norm, table)
        table = jnp.where(lane == k + 4, a, table)
        return total(new), norm, table

    one = jnp.ones((1, 1), F32)
    _, _, table = lax.fori_loop(
        0, ITERS, product, (total(acc), one, jnp.zeros((8, 128), F32))
    )
    for f in range(2):
        src = pl.multiple_of((core * 2 + f) * ROWS, 8)
        for i in range(NI):
            for j in range(NJ):
                start = (i // 6) * 40 + 18 * f + 6 * j + i % 6
                out_ref[pl.ds(start, 8, stride=160), :] = v[pl.ds(src + (i * NJ + j) * 8, 8), :]
    for s in range(32):
        out_ref[pl.ds(40 * s + 36, 4), :] = table[0:4]


def krylov(place, p, pc, near, far, coef, weights):
    return pl.pallas_call(
        krylov_kernel,
        name="krylov",
        out_shape=jax.ShapeDtypeStruct((32 * 40, 128), F32),
        in_specs=[SMEM] + [VMEM] * 9,
        out_specs=VMEM,
        scratch_shapes=[
            pltpu.VMEM((4 * ROWS, 128), F32),
            pltpu.VMEM((STEPS * ROWS, 128), F32),
            pltpu.VMEM((ROWS, 128), F32),
            pltpu.VMEM((STEPS * ROWS, 128), F32),
        ],
        cost_estimate=pl.CostEstimate(flops=10**9, bytes_accessed=8 * 10**6, transcendentals=0),
    )(place, p, pc, near, far, coef, *(w.reshape(-1, 128) for w in weights))


def small_cg(norms, diag):
    n = len(norms)
    zero = jnp.zeros_like(norms[0])
    off = [ratio(norms[k], norms[k - 1]) for k in range(1, n)]

    def image(p):
        q = []
        for k in range(n + 1):
            s = zero
            if k >= 1:
                s = s + p[k - 1]
            if k < n:
                s = s + diag[k] * p[k]
            if k + 1 < n:
                s = s + off[k] * p[k + 1]
            q.append(s)
        return q

    def dot(p, q):
        s = zero
        for k in range(n):
            s = s + norms[k] * p[k] * q[k]
        return jnp.sum(s, axis=0, keepdims=True)

    residual = [zero + 1.0] + [zero] * n
    direction = list(residual)
    control = [zero] * n
    rr = dot(residual, residual)
    for it in range(ITERS):
        h = image(direction)
        step = rr / dot(direction, h)
        control = [c + step * d for c, d in zip(control, direction)]
        residual = [r - step * x for r, x in zip(residual, h)]
        if it + 1 < ITERS:
            new = dot(residual, residual)
            direction = [r + new / rr * d for r, d in zip(residual, direction)]
            rr = new
    return control, residual


def finish_kernel(place_ref, own_ref, other_ref, spread_ref, back_ref, inc_ref, res_ref, tab, zc, zr):
    core = place_ref[0]
    block = place_ref[1]
    table = own_ref[pl.ds(36, 32, stride=40), :]
    control, residual = small_cg(
        [table[:, k : k + 1] for k in range(ITERS)],
        [table[:, 4 + k : 5 + k] for k in range(ITERS)],
    )
    lane = lax.broadcasted_iota(jnp.int32, (32, 128), 1)
    packed = jnp.zeros((32, 128), F32)
    for k, x in enumerate(control + residual):
        packed = jnp.where(lane == k, x, packed)
    tab[...] = packed
    mine = tab[pl.ds(pl.multiple_of(block * 8, 8), 8), :]

    def combine(pair):
        for m in range(8):
            coef = [mine[m : m + 1, k : k + 1] for k in range(7)]
            vs = []
            for k in range(4):
                if k // 2 == pair:
                    start = (block * 8 + m) * 40 + 18 * (k % 2)
                    vs.append([own_ref[pl.ds(start + 6 * j, 6), :] for j in range(NJ)])
                else:
                    start = m * 40 + 18 * (k % 2)
                    vs.append([other_ref[pl.ds(start + 6 * j, 6), :] for j in range(NJ)])
            for j in range(NJ):
                cols = pl.ds(128 * j, 128)
                zc[pl.ds(6 * m, 6), cols] = (
                    coef[0] * vs[0][j] + coef[1] * vs[1][j] + coef[2] * vs[2][j]
                )
                zr[pl.ds(6 * m, 6), cols] = (
                    coef[3] * vs[0][j]
                    + coef[4] * vs[1][j]
                    + coef[5] * vs[2][j]
                    + coef[6] * vs[3][j]
                )

    @pl.when(core == 0)
    def _():
        combine(0)

    @pl.when(core != 0)
    def _():
        combine(1)

    res = exact_dot(zr[...], back_ref[...])
    for m in range(8):
        res_ref[m] = res[6 * m : 6 * m + 6]
    inc = exact_dot(zc[...], spread_ref[...])
    for c in range(12):
        for e in range(4):
            inc_ref[c, pl.ds(e, 48, stride=4), :] = inc[:, 128 * c : 128 * c + 128]


def finish_body(place_ref, own_ref, other_ref, spread_ref, back_ref, inc_ref, res_ref, tab, zc, zr, wide):
    finish_kernel(place_ref, own_ref, other_ref, spread_ref, back_ref, wide, res_ref, tab, zc, zr)
    for c in range(12):
        inc_ref[:, 128 * c : 128 * c + 128] = wide[c]


def finish(place, own, other, spread, back):
    return pl.pallas_call(
        finish_body,
        name="finish",
        out_shape=(
            jax.ShapeDtypeStruct((192, 1536), F32),
            jax.ShapeDtypeStruct((8, 6, 384), F32),
        ),
        in_specs=[SMEM, VMEM, VMEM, VMEM, VMEM],
        out_specs=(VMEM, VMEM),
        scratch_shapes=[
            pltpu.VMEM((32, 128), F32),
            pltpu.VMEM((48, 384), F32),
            pltpu.VMEM((48, 384), F32),
            pltpu.VMEM((12, 192, 128), F32),
        ],
        cost_estimate=pl.CostEstimate(flops=10**9, bytes_accessed=4 * 10**6, transcendentals=0),
    )(place, own, other.reshape(-1, 128), spread, back)


def on_device(innovations, obs_counts, diffusion, courant):
    core = lax.axis_index("tm_1")
    block = lax.axis_index(TM)
    place = jnp.stack([core, block]).astype(jnp.int32)
    pick, mean, spread, back = matrices()
    swap = lambda x, axis: lax.ppermute(x, axis, SWAP)
    turn = lambda x: lax.all_to_all(x, SPACE, 0, 0, tiled=True)

    chunks, wt = prepare(place, obs_counts, diffusion, courant, pick)
    own = turn(chunks)
    forcing = restrict(innovations.reshape(3, 768, 1536), wt, mean)
    pair = swap(own, "tm_1")
    across = swap(own, "tm_0")
    across_pair = swap(across, "tm_1")
    f = turn(forcing)
    p, coef = rhs_part(place, own, pair, f)
    pc = swap(p, "tm_1")
    half = ROWS // 2
    mine = lax.dynamic_slice_in_dim(p, core * half, half, 0) + lax.dynamic_slice_in_dim(
        pc, core * half, half, 0
    )
    near = swap(mine, "tm_0")
    far = swap(near, "tm_1")
    out = turn(
        krylov(place, p, pc, near, far, coef, (own, pair, across, across_pair)).reshape(32, 40, 128)
    )
    other = swap(
        lax.dynamic_slice_in_dim(out, (block + 1 - 2 * core) * 8, 8, 0), "tm_1"
    )
    increment, residual = finish(place, out.reshape(-1, 128), other, spread, back)
    return (increment.reshape(8, 24, 1536), residual)


def solution(mesh):
    torus = Mesh(
        mesh.devices.reshape(2, 4, 4, 2, 2), ("space_0", "space_1", "space_2", "tm_0", "tm_1")
    )
    return jax.shard_map(
        on_device,
        mesh=torus,
        in_specs=(
            P(TM, None, SPACE, None),
            P(TM, SPACE, None),
            P(None, SPACE, None),
            P(None, SPACE, None),
        ),
        out_specs=(P(TM, SPACE, None), P(TM, SPACE, None)),
        check_vma=False,
    )
```

time: 1260 us -> 137 us (0.11)
  starting transfers between devices: 570 us -> 29 us
  blocking collectives: 472 us -> 27.8 us
  other arithmetic: 89.7 us -> 1.68 us
  local copies, waits for them, and re-layouts: 58.6 us -> 7.67 us
  Pallas kernels: 0 us -> 34.4 us
  waiting for transfers between devices: 52.2 us -> 34.6 us
    ppermute x154 -> x7, starting transfers between devices: 566 us -> 18.7 us  [on_device(): swap = lambda x, axis: lax.ppermute(x, axis, SWAP)]
    psum x25 -> x0, blocking collectives: 451 us -> none  [one_axis_at_a_time(): return functools.reduce(lax.psum, axes, x)]
    reduce_sum x6 -> x0, other arithmetic: 43.9 us -> none  [the longest x1 40.6 us: on_device(): forcing = weights * jnp.mean(blocks, axis=(3, 5))]
    pallas_call x0 -> x5, Pallas kernels: none -> 34.4 us  [the longest x1 15.1 us: krylov(): pl.pallas_call(krylov_kernel, name='krylov', out_shape=jax.ShapeDtypeStru...]
    ppermute x154 -> x7, waiting for transfers between devices: 52.2 us -> 18.2 us  [on_device(): swap = lambda x, axis: lax.ppermute(x, axis, SWAP)]
    convert_element_type x1 -> x0, local copies, waits for them, and re-layouts: 30.1 us -> none  [on_device(): innovations.reshape(step_dev, levels, fine_rows // 4, 4, fine_cols // 4, 4)]
    mul x89 -> x0, other arithmetic: 22.7 us -> none  [the longest x44 13 us: adjoint(): spread = diffusion * state_field]
    all_to_all x1, blocking collectives: 5.43 us -> 27.8 us  [on_device(): turn = lambda x: lax.all_to_all(x, SPACE, 0, 0, tiled=True)]
  transfers between devices with their start and end apart: 155 -> 9, of which waited for: 77 -> 7; matrix products, arithmetic and copies ran while one was open for 1% -> 2% of each run, Pallas kernels for 0% -> 9%
where the time goes in v1:
time: 137 us; the launch traced here: 136 us
  waiting for transfers between devices  34.6 us (25%)
  Pallas kernels  34.4 us (25%)
  starting transfers between devices  29 us (21%)
  blocking collectives  27.8 us (20%)
  local copies, waits for them, and re-layouts  7.67 us (6%)
  other arithmetic  1.68 us (1%)
    all_to_all x1, blocking collectives, on_device(): turn = lambda x: lax.all_to_all(x, SPACE, 0, 0, tiled=True)  27.8 us
    ppermute x7, starting transfers between devices, on_device(): swap = lambda x, axis: lax.ppermute(x, axis, SWAP)  18.7 us
    ppermute x7, waiting for transfers between devices, on_device(): swap = lambda x, axis: lax.ppermute(x, axis, SWAP)  18.2 us
    all_to_all x2, waiting for transfers between devices, on_device(): turn = lambda x: lax.all_to_all(x, SPACE, 0, 0, tiled=True)  16.4 us
    pallas_call x1, Pallas kernels, krylov(): pl.pallas_call(krylov_kernel, name='krylov', out_shape=jax.ShapeDtypeStru...  15.1 us
    all_to_all x2, starting transfers between devices, on_device(): turn = lambda x: lax.all_to_all(x, SPACE, 0, 0, tiled=True)  10.3 us
    pallas_call x1, Pallas kernels, restrict(): pl.pallas_call(restrict_kernel, name='restrict', grid=(4,), out_shape=jax...  7.7 us
    unnamed x17, local copies, waits for them, and re-layouts  6.64 us
  transfers between devices with their start and end apart: 9, of which 7 were waited for; matrix products, arithmetic and copies ran while one was open for 2% of the time, Pallas kernels for 9%

profile of v1, /device:TPU:1, one launch (start us, length us, event | category | flops | bytes accessed | tf_op | source)
XLA Modules:
  0.0 135.9 jit_solution(16309631132729771096)
XLA Ops:
  0.6 1.9 %copy.13.diff_ref = f32[32,6,384]{2,1,0:T(8,128)} copy(f32[32,6,384]{2,0,1:T(8,128)} %param.10) | data formatting | bytes 589824 | tf_op args[2]
  2.5 1.9 %copy.14.cour_ref = f32[32,6,384]{2,1,0:T(8,128)} copy(f32[32,6,384]{2,0,1:T(8,128)} %param.11) | data formatting | bytes 589824 | tf_op args[3]
  4.4 0.6 pad_add_fusion.core_ref.place_ref
  5.1 2.9 %prepare.1 = (f32[32,72,128]{2,1,0:T(8,128)}, f32[3,48,384]{2,1,0:T(8,128)}) custom-call(s32[2]{0:T(128)} %pad_add_fusion.core_ref.place_ref, s32[3,6,384]{2,1,0:T(8,128)} %counts_ref.1, f32[32,6,384]{2,1,0:T(8,128)} %copy.13.diff_ref, f32[32,6,384]{2,1,0:T(8,128)} %copy.14.cour_ref, bf16[384,384]{1,0:T(8,128)(2,1)} %constant.28.clone.pick_ref), custom_call_target="tpu_custom_call" | custom-call | flops 1000000000 | bytes 3000000 | tf_op jit(solution)/shard_map/prepare/pallas_call | solution.py:86
  8.0 27.8 %all_to_all.15 = f32[32,72,128]{2,1,0:T(8,128)S(1)} all-to-all(f32[32,72,128]{2,1,0:T(8,128)} %get-tuple-element.8), channel_id=1, replica_groups=mesh['space_0'=2,'space_1'=4,'space_2'=4,'tm_0'=2,'tm_1'=2] {'space_0','..., dimensions={0} | all-to-all | bytes 2359296 | tf_op jit(solution)/shard_map/all_to_all | solution.py:497
  35.8 0.0 copy-start
  35.8 2.5 %collective-permute-start.4 = (f32[32,72,128]{2,1,0:T(8,128)S(1)}, f32[32,72,128]{2,1,0:T(8,128)S(1)}, u32[]{:S(2)}, u32[]{:S(2)}) collective-permute-start(f32[32,72,128]{2,1,0:T(8,128)S(1)} %all_to_all.15), channel_id=1, source_target_pairs={{0,2},{2,0},{1,3},{3,1},{4,6},{6,4},{5,7},{7,5},{8,10},{10,8},{9,1... | collective-permute-start | bytes 3538952 | tf_op jit(solution)/shard_map/ppermute | solution.py:496
  38.2 2.3 %collective-permute-start = (f32[32,72,128]{2,1,0:T(8,128)S(1)}, f32[32,72,128]{2,1,0:T(8,128)}, u32[]{:S(2)}, u32[]{:S(2)}) collective-permute-start(f32[32,72,128]{2,1,0:T(8,128)S(1)} %all_to_all.15), channel_id=1, source_target_pairs={{0,1},{1,0},{2,3},{3,2},{4,5},{5,4},{6,7},{7,6},{8,9},{9,8},{10,11... | collective-permute-start | bytes 3538952 | tf_op jit(solution)/shard_map/ppermute | solution.py:496
  40.5 7.7 %restrict.1 = f32[32,54,128]{2,1,0:T(8,128)} custom-call(bf16[3,768,1536]{2,1,0:T(8,128)(2,1)} %bitcast.16, f32[3,48,384]{2,1,0:T(8,128)} %get-tuple-element.9.wt_ref, bf16[1536,384]{1,0:T(8,128)(2,1)} %constant.29.clone.mean_ref), custom_call_target="tpu_custom_call" | custom-call | flops 3000000000 | bytes 9000000 | tf_op jit(solution)/shard_map/restrict/pallas_call | solution.py:117
  48.2 0.0 copy-done
  48.3 3.9 %all-to-all-start.1 = ((f32[32,54,128]{2,1,0:T(8,128)}), f32[32,54,128]{2,1,0:T(8,128)S(1)}, u32[]{:S(2)}, u32[]{:S(2)}) async-start(f32[32,54,128]{2,1,0:T(8,128)} %restrict.1), calls=%async_computation.1 | async-start | bytes 1835008 | tf_op jit(solution)/shard_map/all_to_all | solution.py:497
  52.2 10.6 %collective-permute-done.4 = f32[32,72,128]{2,1,0:T(8,128)S(1)} collective-permute-done((f32[32,72,128]{2,1,0:T(8,128)S(1)}, f32[32,72,128]{2,1,0:T(8,128)S(1)}, u32[]{:S(2)}, u32[]{:S(2)}) %collective-permute-start.4) | collective-permute-done | bytes 1179680 | tf_op jit(solution)/shard_map/ppermute | solution.py:496
  62.8 0.0 copy-start.1
  62.8 5.4 %collective-permute-start.5 = (f32[32,72,128]{2,1,0:T(8,128)S(1)}, f32[32,72,128]{2,1,0:T(8,128)}, u32[]{:S(2)}, u32[]{:S(2)}) collective-permute-start(f32[32,72,128]{2,1,0:T(8,128)S(1)} %collective-permute-done.4), channel_id=1, source_target_pairs={{0,1},{1,0},{2,3},{3,2},{4,5},{5,4},{6,7},{7,6},{8,9},{9,8},{10,11... | collective-permute-start | bytes 3538952 | tf_op jit(solution)/shard_map/ppermute | solution.py:496
  68.2 5.3 %all-to-all-done.1 = f32[32,54,128]{2,1,0:T(8,128)S(1)} async-done(((f32[32,54,128]{2,1,0:T(8,128)}), f32[32,54,128]{2,1,0:T(8,128)S(1)}, u32[]{:S(2)}, u32[]{:S(2)}) %all-to-all-start.1) | async-done | bytes 884768 | tf_op jit(solution)/shard_map/all_to_all | solution.py:497
  73.5 1.0 reshape.39.f_ref
  74.5 0.0 collective-permute-done
  74.5 3.9 %rhs_part.1 = (f32[576,128]{1,0:T(8,128)}, f32[1728,128]{1,0:T(8,128)}) custom-call(s32[2]{0:T(128)} %pad_add_fusion.core_ref.place_ref, f32[2304,128]{1,0:T(8,128)} %bitcast.11, f32[2304,128]{1,0:T(8,128)} %bitcast.3.other_ref.w1, f32[1728,128]{1,0:T(8,128)} %reshape.39.f_ref), custom_call_target="tpu_custom_call" | custom-call | flops 1000000000 | bytes 4000000 | tf_op jit(solution)/shard_map/rhs_part/pallas_call | solution.py:241
  78.4 0.0 copy-done.1
  78.4 2.1 %collective-permute-start.1 = (f32[576,128]{1,0:T(8,128)}, f32[576,128]{1,0:T(8,128)S(1)}, u32[]{:S(2)}, u32[]{:S(2)}) collective-permute-start(f32[576,128]{1,0:T(8,128)} %get-tuple-element.10.p_ref), channel_id=1, source_target_pairs={{0,1},{1,0},{2,3},{3,2},{4,5},{5,4},{6,7},{7,6},{8,9},{9,8},{10,11... | collective-permute-start | bytes 884744 | tf_op jit(solution)/shard_map/ppermute | solution.py:496
  80.6 1.4 %collective-permute-done.1.pc_ref = f32[576,128]{1,0:T(8,128)S(1)} collective-permute-done((f32[576,128]{1,0:T(8,128)}, f32[576,128]{1,0:T(8,128)S(1)}, u32[]{:S(2)}, u32[]{:S(2)}) %collective-permute-start.1) | collective-permute-done | bytes 294944 | tf_op jit(solution)/shard_map/ppermute | solution.py:496
  82.0 0.0 copy-start.3
  82.0 1.0 dynamic-slice_add_fusion
  83.0 2.5 %collective-permute-start.2 = (f32[288,128]{1,0:T(8,128)S(1)}, f32[288,128]{1,0:T(8,128)S(1)}, u32[]{:S(2)}, u32[]{:S(2)}) collective-permute-start(f32[288,128]{1,0:T(8,128)S(1)} %dynamic-slice_add_fusion), channel_id=1, source_target_pairs={{0,2},{2,0},{1,3},{3,1},{4,6},{6,4},{5,7},{7,5},{8,10},{10,8},{9,1... | collective-permute-start | bytes 442376 | tf_op jit(solution)/shard_map/ppermute | solution.py:496
  85.6 4.1 %collective-permute-done.2.near_ref = f32[288,128]{1,0:T(8,128)S(1)} collective-permute-done((f32[288,128]{1,0:T(8,128)S(1)}, f32[288,128]{1,0:T(8,128)S(1)}, u32[]{:S(2)}, u32[]{:S(2)}) %collective-permute-start.2) | collective-permute-done | bytes 147488 | tf_op jit(solution)/shard_map/ppermute | solution.py:496
  89.6 0.0 copy-start.4
  89.6 1.2 collective-permute-start.3
  90.9 1.0 collective-permute-done.3.far_ref
  91.9 0.0 copy-start.5
  91.9 0.0 collective-permute-done.5
  91.9 0.0 copy-done.3
  91.9 0.0 copy-done.4
  91.9 0.6 copy-done.5
  92.5 15.1 %krylov.1 = f32[1280,128]{1,0:T(8,128)} custom-call(s32[2]{0:T(128)} %pad_add_fusion.core_ref.place_ref, f32[576,128]{1,0:T(8,128)} %get-tuple-element.10.p_ref, f32[576,128]{1,0:T(8,128)} %copy-done.3, f32[288,128]{1,0:T(8,128)} %copy-done.4, f32[288,128]{1,0:T(8,128)} %copy-done.5, f32[1728,128]{1,0:T(8,128)} %get-tuple-element.11.coef_ref, ...), custom_call_target="tpu_custom_call" | custom-call | flops 1000000000 | bytes 8000000 | tf_op jit(solution)/shard_map/krylov/pallas_call | solution.py:354
  107.7 6.4 %all-to-all-start.2 = ((f32[32,40,128]{2,1,0:T(8,128)}), f32[32,40,128]{2,1,0:T(8,128)S(1)}, u32[]{:S(2)}, u32[]{:S(2)}) async-start(f32[32,40,128]{2,1,0:T(8,128)} %bitcast.13), calls=%async_computation.2 | async-start | bytes 1310720 | tf_op jit(solution)/shard_map/all_to_all | solution.py:497
  114.0 11.1 %all-to-all-done.2 = f32[32,40,128]{2,1,0:T(8,128)S(1)} async-done(((f32[32,40,128]{2,1,0:T(8,128)}), f32[32,40,128]{2,1,0:T(8,128)S(1)}, u32[]{:S(2)}, u32[]{:S(2)}) %all-to-all-start.2) | async-done | bytes 655392 | tf_op jit(solution)/shard_map/all_to_all | solution.py:497
  125.2 0.0 copy-start.2
  125.2 2.7 %collective-permute-start.6 = (f32[8,40,128]{2,1,0:T(8,128)S(1)}, f32[8,40,128]{2,1,0:T(8,128)S(1)}, u32[]{:S(2)}, u32[]{:S(2)}) collective-permute-start(f32[8,40,128]{2,1,0:T(8,128)S(1)} %constant_dynamic-slice_fusion), channel_id=1, source_target_pairs={{0,1},{1,0},{2,3},{3,2},{4,5},{5,4},{6,7},{7,6},{8,9},{9,8},{10,11... | collective-permute-start | bytes 491528 | tf_op jit(solution)/shard_map/ppermute | solution.py:496
  127.9 1.0 collective-permute-done.6
  129.0 0.0 copy-start.6
  129.0 0.0 copy-done.2
  129.0 0.7 copy-done.6
  129.6 4.7 %finish.1 = (f32[192,1536]{1,0:T(8,128)}, f32[8,6,384]{2,1,0:T(8,128)}) custom-call(s32[2]{0:T(128)} %pad_add_fusion.core_ref.place_ref, f32[1280,128]{1,0:T(8,128)} %bitcast.15, f32[320,128]{1,0:T(8,128)} %bitcast.17, bf16[384,1536]{1,0:T(8,128)(2,1)} %constant.30.clone.spread_ref, bf16[384,384]{1,0:T(8,128)(2,1)} %constant.31.clone.back_ref), custom_call_target="tpu_custom_call" | custom-call | flops 1000000000 | bytes 4000000 | tf_op jit(solution)/shard_map/finish/pallas_call | solution.py:472
  134.3 1.5 %copy.15 = f32[8,6,384]{2,0,1:T(8,128)} copy(f32[8,6,384]{2,1,0:T(8,128)} %get-tuple-element.17) | data formatting | bytes 147456
  (1 shorter events, 0.0 us)
Async XLA Ops:
  35.8 12.5 %copy-start = (f32[32,72,128]{2,1,0:T(8,128)}, f32[32,72,128]{2,1,0:T(8,128)S(1)}, u32[]{:S(2)}) copy-start(f32[32,72,128]{2,1,0:T(8,128)S(1)} %all_to_all.15) | copy-start | bytes 3538948
  35.8 27.0 %collective-permute-start.4 = (f32[32,72,128]{2,1,0:T(8,128)S(1)}, f32[32,72,128]{2,1,0:T(8,128)S(1)}, u32[]{:S(2)}, u32[]{:S(2)}) collective-permute-start(f32[32,72,128]{2,1,0:T(8,128)S(1)} %all_to_all.15), channel_id=1, source_target_pairs={{0,2},{2,0},{1,3},{3,1},{4,6},{6,4},{5,7},{7,5},{8,10},{10,8},{9,1... | collective-permute-start | bytes 3538952 | tf_op jit(solution)/shard_map/ppermute | solution.py:496
  38.2 36.3 %collective-permute-start = (f32[32,72,128]{2,1,0:T(8,128)S(1)}, f32[32,72,128]{2,1,0:T(8,128)}, u32[]{:S(2)}, u32[]{:S(2)}) collective-permute-start(f32[32,72,128]{2,1,0:T(8,128)S(1)} %all_to_all.15), channel_id=1, source_target_pairs={{0,1},{1,0},{2,3},{3,2},{4,5},{5,4},{6,7},{7,6},{8,9},{9,8},{10,11... | collective-permute-start | bytes 3538952 | tf_op jit(solution)/shard_map/ppermute | solution.py:496
  48.3 25.2 %all-to-all-start.1 = ((f32[32,54,128]{2,1,0:T(8,128)}), f32[32,54,128]{2,1,0:T(8,128)S(1)}, u32[]{:S(2)}, u32[]{:S(2)}) async-start(f32[32,54,128]{2,1,0:T(8,128)} %restrict.1), calls=%async_computation.1 | async-start | bytes 1835008 | tf_op jit(solution)/shard_map/all_to_all | solution.py:497
  62.8 15.7 %copy-start.1 = (f32[32,72,128]{2,1,0:T(8,128)}, f32[32,72,128]{2,1,0:T(8,128)S(1)}, u32[]{:S(2)}) copy-start(f32[32,72,128]{2,1,0:T(8,128)S(1)} %collective-permute-done.4) | copy-start | bytes 3538948
  62.8 29.1 %collective-permute-start.5 = (f32[32,72,128]{2,1,0:T(8,128)S(1)}, f32[32,72,128]{2,1,0:T(8,128)}, u32[]{:S(2)}, u32[]{:S(2)}) collective-permute-start(f32[32,72,128]{2,1,0:T(8,128)S(1)} %collective-permute-done.4), channel_id=1, source_target_pairs={{0,1},{1,0},{2,3},{3,2},{4,5},{5,4},{6,7},{7,6},{8,9},{9,8},{10,11... | collective-permute-start | bytes 3538952 | tf_op jit(solution)/shard_map/ppermute | solution.py:496
  78.4 3.5 %collective-permute-start.1 = (f32[576,128]{1,0:T(8,128)}, f32[576,128]{1,0:T(8,128)S(1)}, u32[]{:S(2)}, u32[]{:S(2)}) collective-permute-start(f32[576,128]{1,0:T(8,128)} %get-tuple-element.10.p_ref), channel_id=1, source_target_pairs={{0,1},{1,0},{2,3},{3,2},{4,5},{5,4},{6,7},{7,6},{8,9},{9,8},{10,11... | collective-permute-start | bytes 884744 | tf_op jit(solution)/shard_map/ppermute | solution.py:496
  82.0 9.9 %copy-start.3 = (f32[576,128]{1,0:T(8,128)}, f32[576,128]{1,0:T(8,128)S(1)}, u32[]{:S(2)}) copy-start(f32[576,128]{1,0:T(8,128)S(1)} %collective-permute-done.1.pc_ref) | copy-start | bytes 884740
  83.0 6.6 %collective-permute-start.2 = (f32[288,128]{1,0:T(8,128)S(1)}, f32[288,128]{1,0:T(8,128)S(1)}, u32[]{:S(2)}, u32[]{:S(2)}) collective-permute-start(f32[288,128]{1,0:T(8,128)S(1)} %dynamic-slice_add_fusion), channel_id=1, source_target_pairs={{0,2},{2,0},{1,3},{3,1},{4,6},{6,4},{5,7},{7,5},{8,10},{10,8},{9,1... | collective-permute-start | bytes 442376 | tf_op jit(solution)/shard_map/ppermute | solution.py:496
  89.6 2.2 %copy-start.4 = (f32[288,128]{1,0:T(8,128)}, f32[288,128]{1,0:T(8,128)S(1)}, u32[]{:S(2)}) copy-start(f32[288,128]{1,0:T(8,128)S(1)} %collective-permute-done.2.near_ref) | copy-start | bytes 442372
  89.6 2.2 %collective-permute-start.3 = (f32[288,128]{1,0:T(8,128)S(1)}, f32[288,128]{1,0:T(8,128)S(1)}, u32[]{:S(2)}, u32[]{:S(2)}) collective-permute-start(f32[288,128]{1,0:T(8,128)S(1)} %collective-permute-done.2.near_ref), channel_id=1, source_target_pairs={{0,1},{1,0},{2,3},{3,2},{4,5},{5,4},{6,7},{7,6},{8,9},{9,8},{10,11... | collective-permute-start | bytes 442376 | tf_op jit(solution)/shard_map/ppermute | solution.py:496
  91.9 0.7 copy-start.5
  107.7 17.5 %all-to-all-start.2 = ((f32[32,40,128]{2,1,0:T(8,128)}), f32[32,40,128]{2,1,0:T(8,128)S(1)}, u32[]{:S(2)}, u32[]{:S(2)}) async-start(f32[32,40,128]{2,1,0:T(8,128)} %bitcast.13), calls=%async_computation.2 | async-start | bytes 1310720 | tf_op jit(solution)/shard_map/all_to_all | solution.py:497
  125.2 3.8 %copy-start.2 = (f32[32,40,128]{2,1,0:T(8,128)}, f32[32,40,128]{2,1,0:T(8,128)S(1)}, u32[]{:S(2)}) copy-start(f32[32,40,128]{2,1,0:T(8,128)S(1)} %all-to-all-done.2) | copy-start | bytes 1966084
  125.2 3.8 %collective-permute-start.6 = (f32[8,40,128]{2,1,0:T(8,128)S(1)}, f32[8,40,128]{2,1,0:T(8,128)S(1)}, u32[]{:S(2)}, u32[]{:S(2)}) collective-permute-start(f32[8,40,128]{2,1,0:T(8,128)S(1)} %constant_dynamic-slice_fusion), channel_id=1, source_target_pairs={{0,1},{1,0},{2,3},{3,2},{4,5},{5,4},{6,7},{7,6},{8,9},{9,8},{10,11... | collective-permute-start | bytes 491528 | tf_op jit(solution)/shard_map/ppermute | solution.py:496
  129.0 0.7 copy-start.6

commit v2 on v1

v2 whole, which is shorter than its diff:
```python
import jax
import jax.numpy as jnp
from jax import lax
from jax.experimental import pallas as pl
from jax.experimental.pallas import tpu as pltpu
from jax.sharding import Mesh
from jax.sharding import PartitionSpec as P

SPACE = ("space_0", "space_1", "space_2")
TURN = ("space_2", "space_0", "space_1")
TM = ("tm_0", "tm_1")
SWAP = [(0, 1), (1, 0)]
F32 = jnp.float32
BF16 = jnp.bfloat16

NI, NJ = 24, 3
REGS = NI * NJ
ROWS = REGS * 8
STEPS = 12
ITERS = 3
AT_F, AT_W, WIDTH = 18, 72, 184
FIELD = 24
BACK = 40
VMEM = pl.BlockSpec(memory_space=pltpu.VMEM)
SMEM = pl.BlockSpec(memory_space=pltpu.SMEM)
ANY = pl.BlockSpec(memory_space=pl.ANY)


def params(mib):
    return pltpu.CompilerParams(vmem_limit_bytes=mib * 2**20)


def cost(us):
    return pl.CostEstimate(flops=int(us * 10**7), bytes_accessed=10**6, transcendentals=0)


def lanes(shape):
    return lax.broadcasted_iota(jnp.int32, shape, 1)


def pick(index, blocks, which, shape):
    out = None
    for k, x in enumerate(blocks):
        y = jnp.take_along_axis(x, index, axis=1, mode="promise_in_bounds")
        out = y if out is None else jnp.where(which == k, y, out)
    return out


def to_held(blocks):
    shape = blocks[0].shape
    out = []
    for j in range(NJ):
        column = lanes(shape) * NJ + j
        out.append(pick(column & 127, blocks, column >> 7, shape))
    return out


def to_natural(held, b, repeat):
    shape = held[0].shape
    column = (lanes(shape) + 128 * b) // repeat
    lane = (column * 43691) >> 17
    return pick(lane, held, column - lane * NJ, shape)


def scatter_kernel(
    place_ref, counts_ref, across_ref, diff_ref, cour_ref, fine_ref, out_ref, mean_ref, sums_ref, w_ref
):
    @pl.when(pl.program_id(0) == 0)
    def _():
        shape = (512, 128)
        row = lax.broadcasted_iota(jnp.int32, shape, 0)
        mean_ref[...] = jnp.where((row >> 2) == lanes(shape), 1.0 / 16.0, 0.0).astype(BF16)
        for half, ref in enumerate((counts_ref, across_ref)):
            for t in range(3):
                w = to_held([ref[t, :, 128 * b : 128 * b + 128].astype(F32) for b in range(3)])
                for j in range(NJ):
                    w_ref[pl.ds((half * 3 + t) * 24 + 8 * j, 6), :] = w[j]

    def store(row, value):
        out_ref[pl.ds(row, 8, stride=WIDTH), :] = value

    core = place_ref[0]
    for i in range(6):
        blocks = [
            jnp.where(
                core == 0,
                diff_ref[i, :, 128 * b : 128 * b + 128],
                cour_ref[i, :, 128 * b : 128 * b + 128],
            )
            for b in range(3)
        ]
        for j, x in enumerate(to_held(blocks)):
            store(6 * j + i, x)
    for t in range(3):
        for b in range(3):
            sums_ref[3 * t + b] = jnp.dot(
                fine_ref[t, :, 512 * b : 512 * b + 512],
                mean_ref[...],
                preferred_element_type=F32,
            )
        for i in range(6):
            blocks = [
                (
                    sums_ref[3 * t + b, pl.ds(4 * i, 8, stride=24), :]
                    + sums_ref[3 * t + b, pl.ds(4 * i + 1, 8, stride=24), :]
                )
                + (
                    sums_ref[3 * t + b, pl.ds(4 * i + 2, 8, stride=24), :]
                    + sums_ref[3 * t + b, pl.ds(4 * i + 3, 8, stride=24), :]
                )
                for b in range(3)
            ]
            for j, x in enumerate(to_held(blocks)):
                row = 6 * j + i
                for half in range(2):
                    w = jnp.broadcast_to(w_ref[pl.ds((half * 3 + t) * 24 + 8 * j + i, 1), :], (8, 128))
                    store(AT_W + (half * 3 + t) * 18 + row, w)
                    if half == 0:
                        store(AT_F + 18 * t + row, w * x)


def scatter(place, counts, across, diffusion, courant, fine):
    return pl.pallas_call(
        scatter_kernel,
        name="scatter",
        grid=(4,),
        out_shape=jax.ShapeDtypeStruct((32 * WIDTH, 128), F32),
        in_specs=[
            SMEM,
            pl.BlockSpec((3, 6, 384), lambda g: (0, 0, 0)),
            pl.BlockSpec((3, 6, 384), lambda g: (0, 0, 0)),
            pl.BlockSpec((6, 8, 384), lambda g: (0, g, 0)),
            pl.BlockSpec((6, 8, 384), lambda g: (0, g, 0)),
            pl.BlockSpec((3, 192, 1536), lambda g: (0, g, 0)),
        ],
        out_specs=pl.BlockSpec((8 * WIDTH, 128), lambda g: (g, 0)),
        scratch_shapes=[
            pltpu.VMEM((512, 128), BF16),
            pltpu.VMEM((9, 192, 128), F32),
            pltpu.VMEM((144, 128), F32),
        ],
        compiler_params=params(24),
        cost_estimate=cost(8),
    )(place, counts, across, diffusion, courant, fine)


def reg(ref, base, i, j):
    return ref[pl.ds((base + i * NJ + j) * 8, 8), :]


def put(ref, base, i, j, value):
    ref[pl.ds((base + i * NJ + j) * 8, 8), :] = value


def taken(ref, width, first, i, j):
    return ref[pl.ds((i // 6) * 8 * width + first + 6 * j + i % 6, 8, stride=width), :]


def edges():
    sub = lax.broadcasted_iota(jnp.int32, (8, 128), 0)
    first, last = sub == 0, sub == 7
    north = lambda x: jnp.where(first, 0.0, pltpu.roll(x, 1, 0))
    south = lambda x: jnp.where(last, 0.0, pltpu.roll(x, 7, 0))
    return north, south


def west(row, j):
    return row[j - 1] if j else pltpu.roll(row[NJ - 1], 1, 1)


def east(row, j):
    return row[j + 1] if j + 1 < NJ else pltpu.roll(row[0], 127, 1)


def tangent_step(src, sb, dst, db, coef):
    north, south = edges()
    load = lambda i: [reg(src, sb, i, j) for j in range(NJ)]
    first, last = load(0), load(NI - 1)
    above = [north(x) for x in last]
    here = first
    for i in range(NI):
        below = load(i + 1) if i + 1 < NI else [south(x) for x in first]
        for j in range(NJ):
            put(
                dst,
                db,
                i,
                j,
                reg(coef, 0, i, j) * here[j]
                + reg(coef, REGS, i, j) * (above[j] + below[j] + east(here, j))
                + reg(coef, 2 * REGS, i, j) * west(here, j),
            )
        above, here = here, below


def adjoint_step(lam, coef, term):
    north, south = edges()

    def load(i):
        y = [reg(lam, 0, i, j) for j in range(NJ)]
        return y, [reg(coef, REGS, i, j) * y[j] for j in range(NJ)]

    above = [north(z) for z in load(NI - 1)[1]]
    y, here = load(0)
    wrap = [south(z) for z in here]
    for i in range(NI):
        y_next, below = load(i + 1) if i + 1 < NI else (None, wrap)
        both = [reg(coef, 2 * REGS, i, j) * y[j] for j in range(NJ)]
        new = [
            reg(coef, 0, i, j) * y[j] + (above[j] + below[j]) + (west(here, j) + east(both, j))
            for j in range(NJ)
        ]
        for j in range(NJ):
            add = term(i, j)
            put(lam, 0, i, j, new[j] if add is None else new[j] + add)
        above, here, y = here, below, y_next


def rhs_kernel(place_ref, own_ref, other_ref, keep_ref, send_ref, coef_ref, lam):
    core = place_ref[0]
    block = place_ref[1]

    def coefficients(diff_ref, diff_width, cour_ref, cour_width):
        for i in range(NI):
            for j in range(NJ):
                d = taken(diff_ref, diff_width, 0, i, j)
                c = taken(cour_ref, cour_width, 0, i, j)
                put(coef_ref, 0, i, j, 1.0 - 4.0 * d - c)
                put(coef_ref, REGS, i, j, d)
                put(coef_ref, 2 * REGS, i, j, d + c)

    @pl.when(core == 0)
    def _():
        coefficients(own_ref, WIDTH, other_ref, FIELD)

    @pl.when(core != 0)
    def _():
        coefficients(other_ref, FIELD, own_ref, WIDTH)

    for i in range(NI):
        for j in range(NJ):
            put(lam, 0, i, j, taken(own_ref, WIDTH, AT_F + 36, i, j))
    for t in (1, 0):
        adjoint_step(lam, coef_ref, lambda i, j, t=t: taken(own_ref, WIDTH, AT_F + 18 * t, i, j))

    def more(_, carry):
        adjoint_step(lam, coef_ref, lambda i, j: None)
        return carry

    lax.fori_loop(0, 3 * block, more, 0)
    half = ROWS // 2
    keep_ref[...] = lam[pl.ds(pl.multiple_of(core * half, 8), half), :]
    send_ref[...] = lam[pl.ds(pl.multiple_of((1 - core) * half, 8), half), :]


def rhs_part(place, own, other):
    return pl.pallas_call(
        rhs_kernel,
        name="rhs_part",
        out_shape=(
            jax.ShapeDtypeStruct((ROWS // 2, 128), F32),
            jax.ShapeDtypeStruct((ROWS // 2, 128), F32),
            jax.ShapeDtypeStruct((3 * ROWS, 128), F32),
        ),
        in_specs=[SMEM, VMEM, VMEM],
        out_specs=(VMEM, VMEM, VMEM),
        scratch_shapes=[pltpu.VMEM((ROWS, 128), F32)],
        compiler_params=params(16),
        cost_estimate=cost(4),
    )(place, own, other.reshape(-1, 128))


def weights_kernel(place_ref, own_ref, pair_ref, out_ref):
    block = place_ref[1]
    for ref, flip in ((own_ref, 0), (pair_ref, 1)):
        for half in range(2):
            base = jnp.bitwise_xor(block, flip + 2 * half) * 3 * REGS
            for t in range(3):
                for i in range(NI):
                    for j in range(NJ):
                        row = pl.multiple_of((base + t * REGS + i * NJ + j) * 8, 8)
                        out_ref[pl.ds(row, 8), :] = taken(
                            ref, WIDTH, AT_W + (3 * half + t) * 18, i, j
                        )


def weights(place, own, pair):
    return pl.pallas_call(
        weights_kernel,
        name="weights",
        out_shape=jax.ShapeDtypeStruct((STEPS * ROWS, 128), F32),
        in_specs=[SMEM, VMEM, VMEM],
        out_specs=VMEM,
        compiler_params=params(24),
        cost_estimate=cost(4),
    )(place, own, pair)


def total(x):
    return jnp.sum(jnp.sum(x, axis=0, keepdims=True), axis=1, keepdims=True)


def ratio(a, b):
    return jnp.where(b > 0.0, a / jnp.where(b > 0.0, b, 1.0), 0.0)


def krylov_kernel(place_ref, mine_ref, other_ref, coef_ref, w_ref, out_ref, v, xs, lam, wbuf, sem):
    core = place_ref[0]
    fetch = pltpu.make_async_copy(w_ref, wbuf, sem)
    fetch.start()
    half = REGS // 2

    def first(lo_ref, hi_ref):
        acc = jnp.zeros((8, 128), F32)
        for r in range(REGS):
            x = (lo_ref if r < half else hi_ref)[pl.ds((r % half) * 8, 8), :]
            v[pl.ds(r * 8, 8), :] = x
            acc = acc + x * x
        lam[pl.ds(0, 8), :] = acc

    @pl.when(core == 0)
    def _():
        first(mine_ref, other_ref)

    @pl.when(core != 0)
    def _():
        first(other_ref, mine_ref)

    norm0 = total(lam[pl.ds(0, 8), :])
    lane = lanes((8, 128))

    def product(k, carry):
        norm, before, table = carry
        base = pl.multiple_of(k * ROWS, 8)
        prev = pl.multiple_of(jnp.maximum(k - 1, 0) * ROWS, 8)
        for r in range(REGS):
            xs[pl.ds(r * 8, 8), :] = v[pl.ds(base + r * 8, 8), :]
        for t in range(STEPS - 1):
            tangent_step(xs, t * REGS, xs, (t + 1) * REGS, coef_ref)

        @pl.when(k == 0)
        def _():
            fetch.wait()

        last = (STEPS - 1) * REGS
        for r in range(REGS):
            lam[pl.ds(r * 8, 8), :] = (
                wbuf[pl.ds((last + r) * 8, 8), :] * xs[pl.ds((last + r) * 8, 8), :]
            )
        for t in range(STEPS - 2, -1, -1):
            adjoint_step(
                lam,
                coef_ref,
                lambda i, j, t=t: reg(wbuf, t * REGS, i, j) * reg(xs, t * REGS, i, j),
            )
        dot = jnp.zeros((8, 128), F32)
        for r in range(REGS):
            x = xs[pl.ds(r * 8, 8), :]
            image = x + lam[pl.ds(r * 8, 8), :]
            lam[pl.ds(r * 8, 8), :] = image
            dot = dot + x * image
        a = ratio(total(dot), norm)
        b = jnp.where(k > 0, ratio(norm, before), 0.0)
        new = jnp.zeros((8, 128), F32)
        for r in range(REGS):
            x = (
                lam[pl.ds(r * 8, 8), :]
                - a * xs[pl.ds(r * 8, 8), :]
                - b * v[pl.ds(prev + r * 8, 8), :]
            )
            v[pl.ds(base + ROWS + r * 8, 8), :] = x
            new = new + x * x
        table = jnp.where(lane == k, norm, table)
        table = jnp.where(lane == k + 4, a, table)
        return total(new), norm, table

    _, _, table = lax.fori_loop(
        0, ITERS, product, (norm0, jnp.ones((1, 1), F32), jnp.zeros((8, 128), F32))
    )
    for f in range(2):
        src = pl.multiple_of((core * 2 + f) * ROWS, 8)
        for i in range(NI):
            for j in range(NJ):
                start = (i // 6) * 8 * BACK + 18 * f + 6 * j + i % 6
                out_ref[pl.ds(start, 8, stride=BACK), :] = v[pl.ds(src + (i * NJ + j) * 8, 8), :]
    for g in range(4):
        out_ref[pl.ds(8 * BACK * g + 36, 8, stride=BACK), :] = table


def krylov(place, mine, other, coef, w):
    return pl.pallas_call(
        krylov_kernel,
        name="krylov",
        out_shape=jax.ShapeDtypeStruct((32 * BACK, 128), F32),
        in_specs=[SMEM, VMEM, VMEM, VMEM, ANY],
        out_specs=VMEM,
        scratch_shapes=[
            pltpu.VMEM((4 * ROWS, 128), F32),
            pltpu.VMEM((STEPS * ROWS, 128), F32),
            pltpu.VMEM((ROWS, 128), F32),
            pltpu.VMEM((STEPS * ROWS, 128), F32),
            pltpu.SemaphoreType.DMA,
        ],
        compiler_params=params(24),
        cost_estimate=cost(12),
    )(place, mine, other, coef, w)


def small_cg(norms, diag):
    n = len(norms)
    zero = jnp.zeros_like(norms[0])
    off = [ratio(norms[k], norms[k - 1]) for k in range(1, n)]

    def image(p):
        q = []
        for k in range(n + 1):
            s = zero
            if k >= 1:
                s = s + p[k - 1]
            if k < n:
                s = s + diag[k] * p[k]
            if k + 1 < n:
                s = s + off[k] * p[k + 1]
            q.append(s)
        return q

    def dot(p, q):
        s = zero
        for k in range(n):
            s = s + norms[k] * p[k] * q[k]
        return jnp.sum(s, axis=0, keepdims=True)

    residual = [zero + 1.0] + [zero] * n
    direction = list(residual)
    control = [zero] * n
    rr = dot(residual, residual)
    for it in range(ITERS):
        h = image(direction)
        step = rr / dot(direction, h)
        control = [c + step * d for c, d in zip(control, direction)]
        residual = [r - step * x for r, x in zip(residual, h)]
        if it + 1 < ITERS:
            new = dot(residual, residual)
            direction = [r + new / rr * d for r, d in zip(residual, direction)]
            rr = new
    return control, residual


def finish_kernel(place_ref, own_ref, other_ref, inc_ref, res_ref, tab, wide):
    core = place_ref[0]
    block = place_ref[1]
    table = own_ref[pl.ds(36, 32, stride=BACK), :]
    control, residual = small_cg(
        [table[:, k : k + 1] for k in range(ITERS)],
        [table[:, 4 + k : 5 + k] for k in range(ITERS)],
    )
    lane = lanes((32, 128))
    packed = jnp.zeros((32, 128), F32)
    for k, x in enumerate(control + residual):
        packed = jnp.where(lane == k, x, packed)
    tab[...] = packed
    mine = tab[pl.ds(pl.multiple_of(block * 8, 8), 8), :]
    coef = [jnp.broadcast_to(mine[:, k : k + 1], (8, 128)) for k in range(7)]
    here = block * 8 * BACK

    def fields(i, j):
        out = []
        for k in range(4):
            row = 18 * (k % 2) + 6 * j + i
            a = own_ref[pl.ds(here + row, 8, stride=BACK), :]
            b = other_ref[pl.ds(row, 8, stride=BACK), :]
            out.append(jnp.where(core == k // 2, a, b))
        return out

    for i in range(6):
        inc, res = [], []
        for j in range(NJ):
            v = fields(i, j)
            inc.append(coef[0] * v[0] + coef[1] * v[1] + coef[2] * v[2])
            res.append(coef[3] * v[0] + coef[4] * v[1] + coef[5] * v[2] + coef[6] * v[3])
        for b in range(3):
            res_ref[i, :, 128 * b : 128 * b + 128] = to_natural(res, b, 1)
        for b in range(12):
            x = to_natural(inc, b, 4)
            for e in range(4):
                wide[b, pl.ds(4 * i + e, 8, stride=24), :] = x
    for b in range(12):
        inc_ref[:, 128 * b : 128 * b + 128] = wide[b]


def finish(place, own, other):
    return pl.pallas_call(
        finish_kernel,
        name="finish",
        out_shape=(
            jax.ShapeDtypeStruct((192, 1536), F32),
            jax.ShapeDtypeStruct((6, 8, 384), F32),
        ),
        in_specs=[SMEM, VMEM, VMEM],
        out_specs=(VMEM, VMEM),
        scratch_shapes=[pltpu.VMEM((32, 128), F32), pltpu.VMEM((12, 192, 128), F32)],
        compiler_params=params(16),
        cost_estimate=cost(3),
    )(place, own, other.reshape(-1, 128))


def on_device(innovations, obs_counts, diffusion, courant):
    core = lax.axis_index("tm_1")
    block = lax.axis_index(TM)
    place = jnp.stack([core, block]).astype(jnp.int32)
    swap = lambda x, axis: lax.ppermute(x, axis, SWAP)
    turn = lambda x: lax.all_to_all(x.reshape(32, -1, 128), TURN, 0, 0, tiled=True)

    own = turn(
        scatter(
            place,
            obs_counts,
            swap(obs_counts, "tm_0"),
            jnp.transpose(diffusion, (1, 0, 2)),
            jnp.transpose(courant, (1, 0, 2)),
            innovations.reshape(3, 768, 1536),
        )
    )
    other = swap(own[:, :FIELD], "tm_1")
    flat = own.reshape(-1, 128)
    pair = swap(flat, "tm_1")
    keep, send, coef = rhs_part(place, flat, other)
    w = weights(place, flat, pair)
    part = keep + swap(send, "tm_1")
    mine = part + swap(part, "tm_0")
    out = turn(krylov(place, mine, swap(mine, "tm_1"), coef, w))
    theirs = swap(lax.dynamic_slice_in_dim(out, (block + 1 - 2 * core) * 8, 8, 0), "tm_1")
    increment, residual = finish(place, out.reshape(-1, 128), theirs)
    return (increment.reshape(8, 24, 1536), jnp.transpose(residual, (1, 0, 2)))


def solution(mesh):
    torus = Mesh(
        mesh.devices.reshape(2, 4, 4, 2, 2), ("space_0", "space_1", "space_2", "tm_0", "tm_1")
    )
    return jax.shard_map(
        on_device,
        mesh=torus,
        in_specs=(
            P(TM, None, SPACE, None),
            P(TM, SPACE, None),
            P(None, SPACE, None),
            P(None, SPACE, None),
        ),
        out_specs=(P(TM, SPACE, None), P(TM, SPACE, None)),
        check_vma=False,
    )
```

time: 137 us -> 116 us (0.85)
  blocking collectives: 27.8 us -> 44.4 us
  starting transfers between devices: 29 us -> 17 us
  Pallas kernels: 34.4 us -> 22.6 us
  waiting for transfers between devices: 34.6 us -> 25.3 us
  local copies, waits for them, and re-layouts: 7.67 us -> 5.74 us
  other arithmetic: 1.68 us -> 0.11 us
    all_to_all x1, blocking collectives: 27.8 us -> 44.4 us  [on_device(): lax.all_to_all(x.reshape(32, -1, 128), TURN, 0, 0, tiled=True)]
    all_to_all x2 -> x1, starting transfers between devices: 10.3 us -> 4.1 us  [on_device(): lax.all_to_all(x.reshape(32, -1, 128), TURN, 0, 0, tiled=True)]
    pallas_call x3, Pallas kernels: 15.3 us -> 9.35 us  [the longest x1 4.33 us: scatter(): pl.pallas_call(scatter_kernel, name='scatter', grid=(4,), out_shape=jax.S...]
    ppermute x7, starting transfers between devices: 18.7 us -> 12.9 us  [on_device(): swap = lambda x, axis: lax.ppermute(x, axis, SWAP)]
    ppermute x7, waiting for transfers between devices: 18.2 us -> 13.5 us  [on_device(): swap = lambda x, axis: lax.ppermute(x, axis, SWAP)]
    all_to_all x2 -> x1, waiting for transfers between devices: 16.4 us -> 11.8 us  [on_device(): lax.all_to_all(x.reshape(32, -1, 128), TURN, 0, 0, tiled=True)]
    pallas_call x1, Pallas kernels: 15.1 us -> 11.8 us  [krylov(): pl.pallas_call(krylov_kernel, name='krylov', out_shape=jax.ShapeDtypeStru...]
    pallas_call x1, Pallas kernels: 3.95 us -> 1.43 us  [rhs_part(): pl.pallas_call(rhs_kernel, name='rhs_part', out_shape=(jax.ShapeDtypeStru...]
  transfers between devices with their start and end apart: 9 -> 8, of which waited for: 7 -> 6; matrix products, arithmetic and copies ran while one was open for 2% -> 0% of each run, Pallas kernels for 9% -> 2%
where the time goes in v2:
time: 116 us
  blocking collectives  44.4 us (38%)
  waiting for transfers between devices  25.3 us (22%)
  Pallas kernels  22.6 us (19%)
  starting transfers between devices  17 us (15%)
  local copies, waits for them, and re-layouts  5.74 us (5%)
    all_to_all x1, blocking collectives, on_device(): lax.all_to_all(x.reshape(32, -1, 128), TURN, 0, 0, tiled=True)  44.4 us
    ppermute x7, waiting for transfers between devices, on_device(): swap = lambda x, axis: lax.ppermute(x, axis, SWAP)  13.5 us
    ppermute x7, starting transfers between devices, on_device(): swap = lambda x, axis: lax.ppermute(x, axis, SWAP)  12.9 us
    pallas_call x1, Pallas kernels, krylov(): pl.pallas_call(krylov_kernel, name='krylov', out_shape=jax.ShapeDtypeStru...  11.8 us
    all_to_all x1, waiting for transfers between devices, on_device(): lax.all_to_all(x.reshape(32, -1, 128), TURN, 0, 0, tiled=True)  11.8 us
    unnamed x8, local copies, waits for them, and re-layouts  5.7 us
    pallas_call x1, Pallas kernels, scatter(): pl.pallas_call(scatter_kernel, name='scatter', grid=(4,), out_shape=jax.S...  4.33 us
    all_to_all x1, starting transfers between devices, on_device(): lax.all_to_all(x.reshape(32, -1, 128), TURN, 0, 0, tiled=True)  4.1 us
  transfers between devices with their start and end apart: 8, of which 6 were waited for; matrix products, arithmetic and copies ran while one was open for 0% of the time, Pallas kernels for 2%

profile of v2, /device:TPU:1, one launch (start us, length us, event | category | flops | bytes accessed | tf_op | source)
XLA Modules:
  0.0 115.9 jit_solution(12298220170400825592)
XLA Ops:
  0.6 3.6 %collective-permute-start = (s32[3,6,384]{2,1,0:T(8,128)}, s32[3,6,384]{2,1,0:T(8,128)S(1)}, u32[]{:S(2)}, u32[]{:S(2)}) collective-permute-start(s32[3,6,384]{2,1,0:T(8,128)} %counts_ref.1), channel_id=1, source_target_pairs={{0,2},{2,0},{1,3},{3,1},{4,6},{6,4},{5,7},{7,5},{8,10},{10,8},{9,1... | collective-permute-start | bytes 82952 | tf_op jit(solution)/shard_map/ppermute | solution.py:511
  4.3 0.1 pad_add_fusion.place_ref
  4.3 1.5 %collective-permute-done.across_ref = s32[3,6,384]{2,1,0:T(8,128)S(1)} collective-permute-done((s32[3,6,384]{2,1,0:T(8,128)}, s32[3,6,384]{2,1,0:T(8,128)S(1)}, u32[]{:S(2)}, u32[]{:S(2)}) %collective-permute-start) | collective-permute-done | bytes 27680 | tf_op jit(solution)/shard_map/ppermute | solution.py:511
  5.8 0.0 copy-start
  5.8 3.0 %copy-done = bf16[3,32,24,1536]{3,2,1,0:T(8,128)(2,1)S(1)} copy-done((bf16[3,32,24,1536]{3,2,1,0:T(8,128)(2,1)S(1)}, bf16[3,32,24,1536]{3,2,1,0:T(8,128)(2,1)}, u32[]{:S(2)}) %copy-start) | copy-done | bytes 7077912
  8.8 0.0 copy-start.1
  8.8 1.0 copy-done.1
  9.8 0.0 copy-start.2
  9.8 1.0 copy-done.2
  10.8 0.0 copy-start.3
  10.8 0.8 copy-done.3
  11.5 4.3 %scatter.1 = f32[5888,128]{1,0:T(8,128)S(1)} custom-call(s32[2]{0:T(128)S(1)} %pad_add_fusion.place_ref, s32[3,6,384]{2,1,0:T(8,128)S(1)} %copy-done.3, s32[3,6,384]{2,1,0:T(8,128)S(1)} %collective-permute-done.across_ref, f32[6,32,384]{2,1,0:T(8,128)S(1)} %bitcast.20, f32[6,32,384]{2,1,0:T(8,128)S(1)} %bitcast.21, bf16[3,768,1536]{2,1,0:T(8,128)(2,1)S(1)} %bitcast.17), custom_call_target="tpu_custom_call" | custom-call | flops 80000000 | bytes 1000000 | tf_op jit(solution)/shard_map/scatter/pallas_call | solution.py:123
  15.9 44.4 %all_to_all.10 = f32[32,184,128]{2,1,0:T(8,128)S(1)} all-to-all(f32[32,184,128]{2,1,0:T(8,128)S(1)} %bitcast.16), channel_id=1, replica_groups=mesh['space_0'=2,'space_1'=4,'space_2'=4,'tm_0'=2,'tm_1'=2] {'space_2','..., dimensions={0} | all-to-all | bytes 6029312 | tf_op jit(solution)/shard_map/all_to_all | solution.py:512
  60.3 3.4 %collective-permute-start.5 = (f32[5888,128]{1,0:T(8,128)S(1)}, f32[5888,128]{1,0:T(8,128)S(1)}, u32[]{:S(2)}, u32[]{:S(2)}) collective-permute-start(f32[5888,128]{1,0:T(8,128)S(1)} %bitcast.13), channel_id=1, source_target_pairs={{0,1},{1,0},{2,3},{3,2},{4,5},{5,4},{6,7},{7,6},{8,9},{9,8},{10,11... | collective-permute-start | bytes 9043976 | tf_op jit(solution)/shard_map/ppermute | solution.py:511
  63.7 0.1 collective-permute-start.1
  63.8 5.5 %collective-permute-done.1 = f32[32,24,128]{2,1,0:T(8,128)S(1)} collective-permute-done((f32[32,24,128]{2,1,0:T(8,128)S(1)}, f32[32,24,128]{2,1,0:T(8,128)S(1)}, u32[]{:S(2)}, u32[]{:S(2)}) %collective-permute-start.1) | collective-permute-done | bytes 393248 | tf_op jit(solution)/shard_map/ppermute | solution.py:511
  69.3 1.4 %rhs_part.1 = (f32[288,128]{1,0:T(8,128)S(1)}, f32[288,128]{1,0:T(8,128)S(1)}, f32[1728,128]{1,0:T(8,128)S(1)}) custom-call(s32[2]{0:T(128)S(1)} %pad_add_fusion.place_ref, f32[5888,128]{1,0:T(8,128)S(1)} %bitcast.14, f32[768,128]{1,0:T(8,128)S(1)} %bitcast.19), custom_call_target="tpu_custom_call" | custom-call | flops 40000000 | bytes 1000000 | tf_op jit(solution)/shard_map/rhs_part/pallas_call | solution.py:257
  70.8 0.1 collective-permute-start.2
  70.9 1.4 %collective-permute-done.2 = f32[288,128]{1,0:T(8,128)S(1)} collective-permute-done((f32[288,128]{1,0:T(8,128)S(1)}, f32[288,128]{1,0:T(8,128)S(1)}, u32[]{:S(2)}, u32[]{:S(2)}) %collective-permute-start.2) | collective-permute-done | bytes 147488 | tf_op jit(solution)/shard_map/ppermute | solution.py:511
  72.2 3.3 %collective-permute-start.3 = (f32[288,128]{1,0:T(8,128)S(1)}, f32[288,128]{1,0:T(8,128)S(1)}, u32[]{:S(2)}, u32[]{:S(2)}) collective-permute-start(f32[288,128]{1,0:T(8,128)S(1)} %add.16), channel_id=1, source_target_pairs={{0,2},{2,0},{1,3},{3,1},{4,6},{6,4},{5,7},{7,5},{8,10},{10,8},{9,1... | collective-permute-start | bytes 442376 | tf_op jit(solution)/shard_map/ppermute | solution.py:511
  75.6 4.1 %collective-permute-done.3 = f32[288,128]{1,0:T(8,128)S(1)} collective-permute-done((f32[288,128]{1,0:T(8,128)S(1)}, f32[288,128]{1,0:T(8,128)S(1)}, u32[]{:S(2)}, u32[]{:S(2)}) %collective-permute-start.3) | collective-permute-done | bytes 147488 | tf_op jit(solution)/shard_map/ppermute | solution.py:511
  79.7 0.8 collective-permute-start.4
  80.5 0.0 collective-permute-done.5.pair_ref
  80.5 1.2 %weights.1.w_ref = f32[6912,128]{1,0:T(8,128)S(1)} custom-call(s32[2]{0:T(128)S(1)} %pad_add_fusion.place_ref, f32[5888,128]{1,0:T(8,128)S(1)} %bitcast.15, f32[5888,128]{1,0:T(8,128)S(1)} %collective-permute-done.5.pair_ref), custom_call_target="tpu_custom_call" | custom-call | flops 40000000 | bytes 1000000 | tf_op jit(solution)/shard_map/weights/pallas_call | solution.py:288
  81.7 0.0 collective-permute-done.4.other_ref
  81.7 11.8 %krylov.1 = f32[1280,128]{1,0:T(8,128)} custom-call(s32[2]{0:T(128)S(1)} %pad_add_fusion.place_ref, f32[288,128]{1,0:T(8,128)S(1)} %add.17.mine_ref, f32[288,128]{1,0:T(8,128)S(1)} %collective-permute-done.4.other_ref, f32[1728,128]{1,0:T(8,128)S(1)} %get-tuple-element.9.coef_ref, f32[6912,128]{1,0:T(8,128)S(1)} %weights.1.w_ref), custom_call_target="tpu_custom_call" | custom-call | flops 120000000 | bytes 1000000 | tf_op jit(solution)/shard_map/krylov/pallas_call | solution.py:391
  93.5 4.1 %all-to-all-start.1 = ((f32[32,40,128]{2,1,0:T(8,128)}), f32[32,40,128]{2,1,0:T(8,128)S(1)}, u32[]{:S(2)}, u32[]{:S(2)}) async-start(f32[32,40,128]{2,1,0:T(8,128)} %bitcast.8), calls=%async_computation.1 | async-start | bytes 1310720 | tf_op jit(solution)/shard_map/all_to_all | solution.py:512
  97.7 11.8 %all-to-all-done.1 = f32[32,40,128]{2,1,0:T(8,128)S(1)} async-done(((f32[32,40,128]{2,1,0:T(8,128)}), f32[32,40,128]{2,1,0:T(8,128)S(1)}, u32[]{:S(2)}, u32[]{:S(2)}) %all-to-all-start.1) | async-done | bytes 655392 | tf_op jit(solution)/shard_map/all_to_all | solution.py:512
  109.5 1.5 %collective-permute-start.6 = (f32[8,40,128]{2,1,0:T(8,128)S(1)}, f32[8,40,128]{2,1,0:T(8,128)S(1)}, u32[]{:S(2)}, u32[]{:S(2)}) collective-permute-start(f32[8,40,128]{2,1,0:T(8,128)S(1)} %constant_dynamic-slice_fusion), channel_id=1, source_target_pairs={{0,1},{1,0},{2,3},{3,2},{4,5},{5,4},{6,7},{7,6},{8,9},{9,8},{10,11... | collective-permute-start | bytes 491528 | tf_op jit(solution)/shard_map/ppermute | solution.py:511
  111.0 1.0 collective-permute-done.6
  112.1 3.8 %finish.1 = (f32[192,1536]{1,0:T(8,128)}, f32[6,8,384]{2,1,0:T(8,128)}) custom-call(s32[2]{0:T(128)S(1)} %pad_add_fusion.place_ref, f32[1280,128]{1,0:T(8,128)S(1)} %bitcast.18, f32[320,128]{1,0:T(8,128)S(1)} %bitcast.22), custom_call_target="tpu_custom_call" | custom-call | flops 30000000 | bytes 1000000 | tf_op jit(solution)/shard_map/finish/pallas_call | solution.py:492
  (4 shorter events, 0.1 us)
Async XLA Ops:
  0.6 5.2 %collective-permute-start = (s32[3,6,384]{2,1,0:T(8,128)}, s32[3,6,384]{2,1,0:T(8,128)S(1)}, u32[]{:S(2)}, u32[]{:S(2)}) collective-permute-start(s32[3,6,384]{2,1,0:T(8,128)} %counts_ref.1), channel_id=1, source_target_pairs={{0,2},{2,0},{1,3},{3,1},{4,6},{6,4},{5,7},{7,5},{8,10},{10,8},{9,1... | collective-permute-start | bytes 82952 | tf_op jit(solution)/shard_map/ppermute | solution.py:511
  5.8 3.0 %copy-start = (bf16[3,32,24,1536]{3,2,1,0:T(8,128)(2,1)S(1)}, bf16[3,32,24,1536]{3,2,1,0:T(8,128)(2,1)}, u32[]{:S(2)}) copy-start(bf16[3,32,24,1536]{3,2,1,0:T(8,128)(2,1)} %param.4) | copy-start | bytes 21233668
  8.8 1.0 copy-start.1
  9.8 1.0 copy-start.2
  10.8 0.8 copy-start.3
  60.3 20.2 %collective-permute-start.5 = (f32[5888,128]{1,0:T(8,128)S(1)}, f32[5888,128]{1,0:T(8,128)S(1)}, u32[]{:S(2)}, u32[]{:S(2)}) collective-permute-start(f32[5888,128]{1,0:T(8,128)S(1)} %bitcast.13), channel_id=1, source_target_pairs={{0,1},{1,0},{2,3},{3,2},{4,5},{5,4},{6,7},{7,6},{8,9},{9,8},{10,11... | collective-permute-start | bytes 9043976 | tf_op jit(solution)/shard_map/ppermute | solution.py:511
  63.7 5.6 %collective-permute-start.1 = (f32[32,24,128]{2,1,0:T(8,128)S(1)}, f32[32,24,128]{2,1,0:T(8,128)S(1)}, u32[]{:S(2)}, u32[]{:S(2)}) collective-permute-start(f32[32,24,128]{2,1,0:T(8,128)S(1)} %slice.4), channel_id=1, source_target_pairs={{0,1},{1,0},{2,3},{3,2},{4,5},{5,4},{6,7},{7,6},{8,9},{9,8},{10,11... | collective-permute-start | bytes 1179656 | tf_op jit(solution)/shard_map/ppermute | solution.py:511
  70.8 1.5 %collective-permute-start.2 = (f32[288,128]{1,0:T(8,128)S(1)}, f32[288,128]{1,0:T(8,128)S(1)}, u32[]{:S(2)}, u32[]{:S(2)}) collective-permute-start(f32[288,128]{1,0:T(8,128)S(1)} %get-tuple-element.8), channel_id=1, source_target_pairs={{0,1},{1,0},{2,3},{3,2},{4,5},{5,4},{6,7},{7,6},{8,9},{9,8},{10,11... | collective-permute-start | bytes 442376 | tf_op jit(solution)/shard_map/ppermute | solution.py:511
  72.2 7.4 %collective-permute-start.3 = (f32[288,128]{1,0:T(8,128)S(1)}, f32[288,128]{1,0:T(8,128)S(1)}, u32[]{:S(2)}, u32[]{:S(2)}) collective-permute-start(f32[288,128]{1,0:T(8,128)S(1)} %add.16), channel_id=1, source_target_pairs={{0,2},{2,0},{1,3},{3,1},{4,6},{6,4},{5,7},{7,5},{8,10},{10,8},{9,1... | collective-permute-start | bytes 442376 | tf_op jit(solution)/shard_map/ppermute | solution.py:511
  79.7 2.0 %collective-permute-start.4 = (f32[288,128]{1,0:T(8,128)S(1)}, f32[288,128]{1,0:T(8,128)S(1)}, u32[]{:S(2)}, u32[]{:S(2)}) collective-permute-start(f32[288,128]{1,0:T(8,128)S(1)} %add.17.mine_ref), channel_id=1, source_target_pairs={{0,1},{1,0},{2,3},{3,2},{4,5},{5,4},{6,7},{7,6},{8,9},{9,8},{10,11... | collective-permute-start | bytes 442376 | tf_op jit(solution)/shard_map/ppermute | solution.py:511
  93.5 15.9 %all-to-all-start.1 = ((f32[32,40,128]{2,1,0:T(8,128)}), f32[32,40,128]{2,1,0:T(8,128)S(1)}, u32[]{:S(2)}, u32[]{:S(2)}) async-start(f32[32,40,128]{2,1,0:T(8,128)} %bitcast.8), calls=%async_computation.1 | async-start | bytes 1310720 | tf_op jit(solution)/shard_map/all_to_all | solution.py:512
  109.5 2.6 %collective-permute-start.6 = (f32[8,40,128]{2,1,0:T(8,128)S(1)}, f32[8,40,128]{2,1,0:T(8,128)S(1)}, u32[]{:S(2)}, u32[]{:S(2)}) collective-permute-start(f32[8,40,128]{2,1,0:T(8,128)S(1)} %constant_dynamic-slice_fusion), channel_id=1, source_target_pairs={{0,1},{1,0},{2,3},{3,2},{4,5},{5,4},{6,7},{7,6},{8,9},{9,8},{10,11... | collective-permute-start | bytes 491528 | tf_op jit(solution)/shard_map/ppermute | solution.py:511

commit v3 on v2

--- a/solution.py
+++ b/solution.py
@@ -18,7 +18,8 @@
 ROWS = REGS * 8
 STEPS = 12
 ITERS = 3
-AT_F, AT_W, WIDTH = 18, 72, 184
+AT_F, WIDTH = 18, 72
+PIECE = 56
 FIELD = 24
 BACK = 40
 VMEM = pl.BlockSpec(memory_space=pltpu.VMEM)
@@ -38,7 +39,7 @@
     return lax.broadcasted_iota(jnp.int32, shape, 1)
 
 
-def pick(index, blocks, which, shape):
+def pick(index, blocks, which):
     out = None
     for k, x in enumerate(blocks):
         y = jnp.take_along_axis(x, index, axis=1, mode="promise_in_bounds")
@@ -51,7 +52,7 @@
     out = []
     for j in range(NJ):
         column = lanes(shape) * NJ + j
-        out.append(pick(column & 127, blocks, column >> 7, shape))
+        out.append(pick(column & 127, blocks, column >> 7))
     return out
 
 
@@ -59,22 +60,37 @@
     shape = held[0].shape
     column = (lanes(shape) + 128 * b) // repeat
     lane = (column * 43691) >> 17
-    return pick(lane, held, column - lane * NJ, shape)
+    return pick(lane, held, column - lane * NJ)
+
+
+def held_kernel(counts_ref, out_ref):
+    for t in range(3):
+        w = to_held([counts_ref[t, :, 128 * b : 128 * b + 128].astype(F32) for b in range(3)])
+        for j in range(NJ):
+            out_ref[pl.ds(18 * t + 6 * j, 6), :] = w[j]
+    out_ref[pl.ds(54, 2), :] = jnp.zeros((2, 128), F32)
+
+
+def held(counts):
+    return pl.pallas_call(
+        held_kernel,
+        name="held",
+        out_shape=jax.ShapeDtypeStruct((PIECE, 128), F32),
+        in_specs=[VMEM],
+        out_specs=VMEM,
+        compiler_params=params(4),
+        cost_estimate=cost(0.5),
+    )(counts)
 
 
 def scatter_kernel(
-    place_ref, counts_ref, across_ref, diff_ref, cour_ref, fine_ref, out_ref, mean_ref, sums_ref, w_ref
+    place_ref, w_ref, diff_ref, cour_ref, fine_ref, out_ref, mean_ref, sums_ref
 ):
     @pl.when(pl.program_id(0) == 0)
     def _():
         shape = (512, 128)
         row = lax.broadcasted_iota(jnp.int32, shape, 0)
         mean_ref[...] = jnp.where((row >> 2) == lanes(shape), 1.0 / 16.0, 0.0).astype(BF16)
-        for half, ref in enumerate((counts_ref, across_ref)):
-            for t in range(3):
-                w = to_held([ref[t, :, 128 * b : 128 * b + 128].astype(F32) for b in range(3)])
-                for j in range(NJ):
-                    w_ref[pl.ds((half * 3 + t) * 24 + 8 * j, 6), :] = w[j]
 
     def store(row, value):
         out_ref[pl.ds(row, 8, stride=WIDTH), :] = value
@@ -111,15 +127,12 @@
                 for b in range(3)
             ]
             for j, x in enumerate(to_held(blocks)):
-                row = 6 * j + i
-                for half in range(2):
-                    w = jnp.broadcast_to(w_ref[pl.ds((half * 3 + t) * 24 + 8 * j + i, 1), :], (8, 128))
-                    store(AT_W + (half * 3 + t) * 18 + row, w)
-                    if half == 0:
-                        store(AT_F + 18 * t + row, w * x)
-
-
-def scatter(place, counts, across, diffusion, courant, fine):
+                row = 18 * t + 6 * j + i
+                w = jnp.broadcast_to(w_ref[pl.ds(row, 1), :], (8, 128))
+                store(AT_F + row, w * x)
+
+
+def scatter(place, w, diffusion, courant, fine):
     return pl.pallas_call(
         scatter_kernel,
         name="scatter",
@@ -127,8 +140,7 @@
         out_shape=jax.ShapeDtypeStruct((32 * WIDTH, 128), F32),
         in_specs=[
             SMEM,
-            pl.BlockSpec((3, 6, 384), lambda g: (0, 0, 0)),
-            pl.BlockSpec((3, 6, 384), lambda g: (0, 0, 0)),
+            pl.BlockSpec((PIECE, 128), lambda g: (0, 0)),
             pl.BlockSpec((6, 8, 384), lambda g: (0, g, 0)),
             pl.BlockSpec((6, 8, 384), lambda g: (0, g, 0)),
             pl.BlockSpec((3, 192, 1536), lambda g: (0, g, 0)),
@@ -137,11 +149,10 @@
         scratch_shapes=[
             pltpu.VMEM((512, 128), BF16),
             pltpu.VMEM((9, 192, 128), F32),
-            pltpu.VMEM((144, 128), F32),
         ],
-        compiler_params=params(24),
+        compiler_params=params(57),
         cost_estimate=cost(8),
-    )(place, counts, across, diffusion, courant, fine)
+    )(place, w, diffusion, courant, fine)
 
 
 def reg(ref, base, i, j):
@@ -270,30 +281,56 @@
     )(place, own, other.reshape(-1, 128))
 
 
-def weights_kernel(place_ref, own_ref, pair_ref, out_ref):
-    block = place_ref[1]
-    for ref, flip in ((own_ref, 0), (pair_ref, 1)):
-        for half in range(2):
-            base = jnp.bitwise_xor(block, flip + 2 * half) * 3 * REGS
-            for t in range(3):
-                for i in range(NI):
-                    for j in range(NJ):
-                        row = pl.multiple_of((base + t * REGS + i * NJ + j) * 8, 8)
-                        out_ref[pl.ds(row, 8), :] = taken(
-                            ref, WIDTH, AT_W + (3 * half + t) * 18, i, j
-                        )
-
-
-def weights(place, own, pair):
+def weights_kernel(place_ref, *refs):
+    out_ref = refs[-1]
+    block, row = place_ref[1], place_ref[2]
+    for core in range(2):
+        for d in range(4):
+            ref = refs[4 * core + d]
+            first = jnp.bitwise_and(row + d, 3) * 6 * NJ
+            for half in range(2):
+                base = jnp.bitwise_xor(block, core + 2 * half) * 3 * REGS + first
+                for t in range(3):
+                    for i in range(6):
+                        for j in range(NJ):
+                            at = pl.multiple_of((base + t * REGS + i * NJ + j) * 8, 8)
+                            start = PIECE * half + 18 * t + 6 * j + i
+                            out_ref[pl.ds(at, 8), :] = ref[pl.ds(start, 8, stride=2 * PIECE), :]
+
+
+def weights(place, pieces):
     return pl.pallas_call(
         weights_kernel,
         name="weights",
         out_shape=jax.ShapeDtypeStruct((STEPS * ROWS, 128), F32),
-        in_specs=[SMEM, VMEM, VMEM],
+        in_specs=[SMEM] + [VMEM] * 8,
         out_specs=VMEM,
-        compiler_params=params(24),
+        compiler_params=params(16),
         cost_estimate=cost(4),
-    )(place, own, pair)
+    )(place, *pieces)
+
+
+def shift(x, axis, by):
+    return lax.ppermute(x, axis, [(k, (k + by) % 4) for k in range(4)])
+
+
+def swap(x, axis):
+    return lax.ppermute(x, axis, SWAP)
+
+
+def crossed(w):
+    both = lax.ppermute(w, ("space_0", "tm_0"), [(k, 3 - k) for k in range(4)])
+    x = jnp.concatenate([w, swap(w, "tm_0")], 0)
+    y = jnp.concatenate([swap(w, "space_0"), both], 0)
+    low = lax.axis_index("space_0") == 0
+    return jnp.stack([jnp.where(low, x, y), jnp.where(low, y, x)])
+
+
+def lined(x):
+    behind, ahead, far = (shift(x, "space_1", by) for by in (1, -1, 2))
+    around = jnp.stack([x, ahead, far, behind, x, ahead, far, behind], 1)
+    start = jnp.bitwise_and(4 - lax.axis_index("space_1"), 3)
+    return lax.dynamic_slice_in_dim(around, start, 4, 1).reshape(2, -1, 128)
 
 
 def total(x):
@@ -507,27 +544,31 @@
 def on_device(innovations, obs_counts, diffusion, courant):
     core = lax.axis_index("tm_1")
     block = lax.axis_index(TM)
-    place = jnp.stack([core, block]).astype(jnp.int32)
-    swap = lambda x, axis: lax.ppermute(x, axis, SWAP)
+    place = jnp.stack([core, block, lax.axis_index("space_2")]).astype(jnp.int32)
     turn = lambda x: lax.all_to_all(x.reshape(32, -1, 128), TURN, 0, 0, tiled=True)
-
-    own = turn(
-        scatter(
-            place,
-            obs_counts,
-            swap(obs_counts, "tm_0"),
-            jnp.transpose(diffusion, (1, 0, 2)),
-            jnp.transpose(courant, (1, 0, 2)),
-            innovations.reshape(3, 768, 1536),
-        )
+    rows = lambda x: x.reshape(-1, 128)
+
+    w = held(obs_counts)
+    cross, w = lax.optimization_barrier((crossed(w), w))
+    chunks = scatter(
+        place,
+        w,
+        jnp.transpose(diffusion, (1, 0, 2)),
+        jnp.transpose(courant, (1, 0, 2)),
+        innovations.reshape(3, 768, 1536),
     )
-    other = swap(own[:, :FIELD], "tm_1")
-    flat = own.reshape(-1, 128)
-    pair = swap(flat, "tm_1")
-    keep, send, coef = rhs_part(place, flat, other)
-    w = weights(place, flat, pair)
+    line, chunks = lax.optimization_barrier((lined(cross), chunks))
+    own = turn(chunks)
+    behind, ahead = shift(line, "space_2", 1), shift(line, "space_2", -1)
+    field = own[:, :FIELD]
+    other = swap(field, "tm_1")
+    keep, send, coef = rhs_part(place, rows(own), other)
     part = keep + swap(send, "tm_1")
-    mine = part + swap(part, "tm_0")
+    near = swap(part, "tm_0")
+    far = (shift(behind[0], "space_2", 1), shift(ahead[1], "space_2", -1))
+    pieces = [rows(x) for x in (line, ahead, jnp.stack(far), behind)]
+    w = weights(place, pieces + [swap(x, "tm_1") for x in pieces])
+    mine = part + near
     out = turn(krylov(place, mine, swap(mine, "tm_1"), coef, w))
     theirs = swap(lax.dynamic_slice_in_dim(out, (block + 1 - 2 * core) * 8, 8, 0), "tm_1")
     increment, residual = finish(place, out.reshape(-1, 128), theirs)

time: 116 us -> 115 us (level)
  blocking collectives: 44.4 us -> 0 us
  starting transfers between devices: 17 us -> 41.2 us
  waiting for transfers between devices: 25.3 us -> 45.6 us
  local copies, waits for them, and re-layouts: 5.74 us -> 0.99 us
  Pallas kernels: 22.6 us -> 25.5 us
    all_to_all x1 -> x0, blocking collectives: 44.4 us -> none  [on_device(): lax.all_to_all(x.reshape(32, -1, 128), TURN, 0, 0, tiled=True)]
    ppermute x7 -> x19, waiting for transfers between devices: 13.5 us -> 33.7 us  [the longest x7 23.8 us: shift(): return lax.ppermute(x, axis, [(k, (k + by) % 4) for k in range(4)])]
    ppermute x7 -> x19, starting transfers between devices: 12.9 us -> 26.7 us  [the longest x7 11.7 us: shift(): return lax.ppermute(x, axis, [(k, (k + by) % 4) for k in range(4)])]
    all_to_all x1 -> x2, starting transfers between devices: 4.1 us -> 14.5 us  [on_device(): lax.all_to_all(x.reshape(32, -1, 128), TURN, 0, 0, tiled=True)]
    unnamed x8 -> x13, local copies, waits for them, and re-layouts: 5.7 us -> 0.84 us
    pallas_call x1, Pallas kernels: 4.33 us -> 6.51 us  [scatter(): pl.pallas_call(scatter_kernel, name='scatter', grid=(4,), out_shape=jax.S...]
    all_to_all x1 -> x2, waiting for transfers between devices: 11.8 us -> 11.9 us  [on_device(): lax.all_to_all(x.reshape(32, -1, 128), TURN, 0, 0, tiled=True)]
  transfers between devices with their start and end apart: 8 -> 21, of which waited for: 6 -> 9; matrix products, arithmetic and copies ran while one was open for 0% -> 1% of each run, Pallas kernels for 2% -> 8%
where the time goes in v3:
time: 115 us
  waiting for transfers between devices  45.6 us (40%)
  starting transfers between devices  41.2 us (36%)
  Pallas kernels  25.5 us (22%)
    ppermute x7, waiting for transfers between devices, shift(): return lax.ppermute(x, axis, [(k, (k + by) % 4) for k in range(4)])  23.8 us
    all_to_all x2, starting transfers between devices, on_device(): lax.all_to_all(x.reshape(32, -1, 128), TURN, 0, 0, tiled=True)  14.5 us
    pallas_call x1, Pallas kernels, krylov(): pl.pallas_call(krylov_kernel, name='krylov', out_shape=jax.ShapeDtypeStru...  12 us
    all_to_all x2, waiting for transfers between devices, on_device(): lax.all_to_all(x.reshape(32, -1, 128), TURN, 0, 0, tiled=True)  11.9 us
    ppermute x7, starting transfers between devices, shift(): return lax.ppermute(x, axis, [(k, (k + by) % 4) for k in range(4)])  11.7 us
    ppermute x11, starting transfers between devices, swap(): return lax.ppermute(x, axis, SWAP)  11.6 us
    ppermute x11, waiting for transfers between devices, swap(): return lax.ppermute(x, axis, SWAP)  9.82 us
    pallas_call x1, Pallas kernels, scatter(): pl.pallas_call(scatter_kernel, name='scatter', grid=(4,), out_shape=jax.S...  6.51 us
  transfers between devices with their start and end apart: 21, of which 9 were waited for; matrix products, arithmetic and copies ran while one was open for 1% of the time, Pallas kernels for 8%

profile of v3, /device:TPU:1, one launch (start us, length us, event | category | flops | bytes accessed | tf_op | source)
XLA Modules:
  0.0 114.9 jit_solution(7279008043138410234)
XLA Ops:
  0.6 0.0 copy-start.1
  0.6 0.8 copy-done.1
  1.4 0.1 held.1.w_ref
  1.5 0.0 copy-start
  1.5 3.4 %collective-permute-start.2 = (f32[56,128]{1,0:T(8,128)S(1)}, f32[56,128]{1,0:T(8,128)S(1)}, u32[]{:S(2)}, u32[]{:S(2)}) collective-permute-start(f32[56,128]{1,0:T(8,128)S(1)} %held.1.w_ref), channel_id=1, source_target_pairs={{0,66},{2,64},{64,2},{66,0},{1,67},{3,65},{65,3},{67,1},{4,70},{6,... | collective-permute-start | bytes 86024 | tf_op jit(solution)/shard_map/ppermute | solution.py:322
  4.9 0.0 collective-permute-start.1
  4.9 1.3 %collective-permute-start = (f32[56,128]{1,0:T(8,128)S(1)}, f32[56,128]{1,0:T(8,128)S(1)}, u32[]{:S(2)}, u32[]{:S(2)}) collective-permute-start(f32[56,128]{1,0:T(8,128)S(1)} %held.1.w_ref), channel_id=1, source_target_pairs={{0,2},{2,0},{1,3},{3,1},{4,6},{6,4},{5,7},{7,5},{8,10},{10,8},{9,1... | collective-permute-start | bytes 86024 | tf_op jit(solution)/shard_map/ppermute | solution.py:318
  6.2 0.6 pad_add_fusion.place_ref
  6.8 0.0 collective-permute-done.2
  6.8 0.9 collective-permute-done.1
  7.7 1.5 %collective-permute-done = f32[56,128]{1,0:T(8,128)S(1)} collective-permute-done((f32[56,128]{1,0:T(8,128)S(1)}, f32[56,128]{1,0:T(8,128)S(1)}, u32[]{:S(2)}, u32[]{:S(2)}) %collective-permute-start) | collective-permute-done | bytes 28704 | tf_op jit(solution)/shard_map/ppermute | solution.py:318
  9.2 1.8 %collective-permute-start.5 = (f32[2,112,128]{2,1,0:T(8,128)S(1)}, f32[2,112,128]{2,1,0:T(8,128)S(1)}, u32[]{:S(2)}, u32[]{:S(2)}) collective-permute-start(f32[2,112,128]{2,1,0:T(8,128)S(1)} %pad_maximum_fusion.1), channel_id=1, source_target_pairs={{0,16},{16,32},{32,48},{48,0},{1,17},{17,33},{33,49},{49,1},{2,18}... | collective-permute-start | bytes 344072 | tf_op jit(solution)/shard_map/ppermute | solution.py:314
  11.0 3.3 %collective-permute-start.4 = (f32[2,112,128]{2,1,0:T(8,128)S(1)}, f32[2,112,128]{2,1,0:T(8,128)S(1)}, u32[]{:S(2)}, u32[]{:S(2)}) collective-permute-start(f32[2,112,128]{2,1,0:T(8,128)S(1)} %pad_maximum_fusion.1), channel_id=1, source_target_pairs={{0,32},{16,48},{32,0},{48,16},{1,33},{17,49},{33,1},{49,17},{2,34}... | collective-permute-start | bytes 344072 | tf_op jit(solution)/shard_map/ppermute | solution.py:314
  14.3 0.7 collective-permute-start.3
  15.1 0.0 copy-done
  15.1 6.5 %scatter.1 = f32[2304,128]{1,0:T(8,128)} custom-call(s32[3]{0:T(128)} %pad_add_fusion.place_ref, f32[56,128]{1,0:T(8,128)} %copy-done, f32[6,32,384]{2,1,0:T(8,128)} %bitcast.57, f32[6,32,384]{2,1,0:T(8,128)} %bitcast.58, bf16[3,768,1536]{2,1,0:T(8,128)(2,1)} %bitcast.56), custom_call_target="tpu_custom_call" | custom-call | flops 80000000 | bytes 1000000 | tf_op jit(solution)/shard_map/scatter/pallas_call | solution.py:136
  21.6 0.0 collective-permute-done.3
  21.6 0.0 collective-permute-done.4
  21.6 0.0 collective-permute-done.5
  21.8 6.1 %all-to-all-start = ((f32[32,72,128]{2,1,0:T(8,128)}), f32[32,72,128]{2,1,0:T(8,128)S(1)}, u32[]{:S(2)}, u32[]{:S(2)}) async-start(f32[32,72,128]{2,1,0:T(8,128)} %bitcast.15), calls=%async_computation | async-start | bytes 2359296 | tf_op jit(solution)/shard_map/all_to_all | solution.py:548
  27.9 1.3 %collective-permute-start.11 = (f32[2,448,128]{2,1,0:T(8,128)S(1)}, f32[2,448,128]{2,1,0:T(8,128)S(1)}, u32[]{:S(2)}, u32[]{:S(2)}) collective-permute-start(f32[2,448,128]{2,1,0:T(8,128)S(1)} %bitcast.43), channel_id=1, source_target_pairs={{0,4},{4,8},{8,12},{12,0},{1,5},{5,9},{9,13},{13,1},{2,6},{6,10},{... | collective-permute-start | bytes 1376264 | tf_op jit(solution)/shard_map/ppermute | solution.py:314
  29.2 1.4 %collective-permute-start.10 = (f32[2,448,128]{2,1,0:T(8,128)S(1)}, f32[2,448,128]{2,1,0:T(8,128)S(1)}, u32[]{:S(2)}, u32[]{:S(2)}) collective-permute-start(f32[2,448,128]{2,1,0:T(8,128)S(1)} %bitcast.44), channel_id=1, source_target_pairs={{0,12},{4,0},{8,4},{12,8},{1,13},{5,1},{9,5},{13,9},{2,14},{6,2},{... | collective-permute-start | bytes 1376264 | tf_op jit(solution)/shard_map/ppermute | solution.py:314
  30.7 22.1 %collective-permute-done.11 = f32[2,448,128]{2,1,0:T(8,128)S(1)} collective-permute-done((f32[2,448,128]{2,1,0:T(8,128)S(1)}, f32[2,448,128]{2,1,0:T(8,128)S(1)}, u32[]{:S(2)}, u32[]{:S(2)}) %collective-permute-start.11) | collective-permute-done | bytes 458784 | tf_op jit(solution)/shard_map/ppermute | solution.py:314
  52.8 0.0 copy-start.2
  52.8 0.1 collective-permute-start.12
  52.9 0.0 all-to-all-done
  52.9 1.9 %collective-permute-start.6 = (f32[32,24,128]{2,1,0:T(8,128)S(1)}, f32[32,24,128]{2,1,0:T(8,128)S(1)}, u32[]{:S(2)}, u32[]{:S(2)}) collective-permute-start(f32[32,24,128]{2,1,0:T(8,128)S(1)} %slice.12), channel_id=1, source_target_pairs={{0,1},{1,0},{2,3},{3,2},{4,5},{5,4},{6,7},{7,6},{8,9},{9,8},{10,11... | collective-permute-start | bytes 1179656 | tf_op jit(solution)/shard_map/ppermute | solution.py:318
  54.8 0.0 collective-permute-done.10
  54.9 3.0 %collective-permute-start.13 = (f32[448,128]{1,0:T(8,128)S(1)}, f32[448,128]{1,0:T(8,128)S(1)}, u32[]{:S(2)}, u32[]{:S(2)}) collective-permute-start(f32[448,128]{1,0:T(8,128)S(1)} %slice_bitcast_fusion), channel_id=1, source_target_pairs={{0,12},{4,0},{8,4},{12,8},{1,13},{5,1},{9,5},{13,9},{2,14},{6,2},{... | collective-permute-start | bytes 688136 | tf_op jit(solution)/shard_map/ppermute | solution.py:314
  57.9 0.3 collective-permute-start.14
  58.2 0.2 collective-permute-start.17
  58.4 1.0 collective-permute-done.12
  59.4 2.7 %collective-permute-start.15 = (f32[896,128]{1,0:T(8,128)S(1)}, f32[896,128]{1,0:T(8,128)S(1)}, u32[]{:S(2)}, u32[]{:S(2)}) collective-permute-start(f32[896,128]{1,0:T(8,128)S(1)} %bitcast.51), channel_id=1, source_target_pairs={{0,1},{1,0},{2,3},{3,2},{4,5},{5,4},{6,7},{7,6},{8,9},{9,8},{10,11... | collective-permute-start | bytes 1376264 | tf_op jit(solution)/shard_map/ppermute | solution.py:318
  62.1 0.7 collective-permute-done.13
  62.8 1.0 collective-permute-start.16
  63.8 0.0 collective-permute-done.6
  63.8 0.0 copy-done.2
  63.8 1.4 %rhs_part.1 = (f32[288,128]{1,0:T(8,128)S(1)}, f32[288,128]{1,0:T(8,128)S(1)}, f32[1728,128]{1,0:T(8,128)S(1)}) custom-call(s32[3]{0:T(128)S(1)} %copy-done.2, f32[2304,128]{1,0:T(8,128)S(1)} %bitcast.41, f32[768,128]{1,0:T(8,128)S(1)} %bitcast.53), custom_call_target="tpu_custom_call" | custom-call | flops 40000000 | bytes 1000000 | tf_op jit(solution)/shard_map/rhs_part/pallas_call | solution.py:268
  65.2 0.1 collective-permute-start.7
  65.3 1.4 %collective-permute-done.7 = f32[288,128]{1,0:T(8,128)S(1)} collective-permute-done((f32[288,128]{1,0:T(8,128)S(1)}, f32[288,128]{1,0:T(8,128)S(1)}, u32[]{:S(2)}, u32[]{:S(2)}) %collective-permute-start.7) | collective-permute-done | bytes 147488 | tf_op jit(solution)/shard_map/ppermute | solution.py:318
  66.7 1.8 %collective-permute-start.8 = (f32[288,128]{1,0:T(8,128)S(1)}, f32[288,128]{1,0:T(8,128)S(1)}, u32[]{:S(2)}, u32[]{:S(2)}) collective-permute-start(f32[288,128]{1,0:T(8,128)S(1)} %add.20), channel_id=1, source_target_pairs={{0,2},{2,0},{1,3},{3,1},{4,6},{6,4},{5,7},{7,5},{8,10},{10,8},{9,1... | collective-permute-start | bytes 442376 | tf_op jit(solution)/shard_map/ppermute | solution.py:318
  68.5 5.1 %collective-permute-done.8 = f32[288,128]{1,0:T(8,128)S(1)} collective-permute-done((f32[288,128]{1,0:T(8,128)S(1)}, f32[288,128]{1,0:T(8,128)S(1)}, u32[]{:S(2)}, u32[]{:S(2)}) %collective-permute-start.8) | collective-permute-done | bytes 147488 | tf_op jit(solution)/shard_map/ppermute | solution.py:318
  73.6 1.1 collective-permute-start.9
  74.7 0.0 collective-permute-done.14.refs_4_
  74.7 0.0 collective-permute-done.17.refs_7_
  74.7 0.0 collective-permute-done.15.refs_5_
  74.7 0.0 collective-permute-done.16.refs_6_
  74.7 1.7 %weights.1.w_ref = f32[6912,128]{1,0:T(8,128)S(1)} custom-call(s32[3]{0:T(128)S(1)} %copy-done.2, f32[896,128]{1,0:T(8,128)S(1)} %bitcast.46, f32[896,128]{1,0:T(8,128)S(1)} %bitcast.52, f32[896,128]{1,0:T(8,128)S(1)} %bitcast.48, f32[896,128]{1,0:T(8,128)S(1)} %bitcast.50, f32[896,128]{1,0:T(8,128)S(1)} %collective-permute-done.14.refs_4_, ...), custom_call_target="tpu_custom_call" | custom-call | flops 40000000 | bytes 1000000 | tf_op jit(solution)/shard_map/weights/pallas_call | solution.py:302
  76.4 0.0 collective-permute-done.9.other_ref
  76.4 12.0 %krylov.1 = f32[1280,128]{1,0:T(8,128)} custom-call(s32[3]{0:T(128)S(1)} %copy-done.2, f32[288,128]{1,0:T(8,128)S(1)} %add.21.mine_ref, f32[288,128]{1,0:T(8,128)S(1)} %collective-permute-done.9.other_ref, f32[1728,128]{1,0:T(8,128)S(1)} %get-tuple-element.16.coef_ref, f32[6912,128]{1,0:T(8,128)S(1)} %weights.1.w_ref), custom_call_target="tpu_custom_call" | custom-call | flops 120000000 | bytes 1000000 | tf_op jit(solution)/shard_map/krylov/pallas_call | solution.py:428
  88.4 8.4 %all-to-all-start.1 = ((f32[32,40,128]{2,1,0:T(8,128)}), f32[32,40,128]{2,1,0:T(8,128)S(1)}, u32[]{:S(2)}, u32[]{:S(2)}) async-start(f32[32,40,128]{2,1,0:T(8,128)} %bitcast.26), calls=%async_computation.1 | async-start | bytes 1310720 | tf_op jit(solution)/shard_map/all_to_all | solution.py:548
  96.8 11.9 %all-to-all-done.1 = f32[32,40,128]{2,1,0:T(8,128)S(1)} async-done(((f32[32,40,128]{2,1,0:T(8,128)}), f32[32,40,128]{2,1,0:T(8,128)S(1)}, u32[]{:S(2)}, u32[]{:S(2)}) %all-to-all-start.1) | async-done | bytes 655392 | tf_op jit(solution)/shard_map/all_to_all | solution.py:548
  108.7 1.3 %collective-permute-start.18 = (f32[8,40,128]{2,1,0:T(8,128)S(1)}, f32[8,40,128]{2,1,0:T(8,128)S(1)}, u32[]{:S(2)}, u32[]{:S(2)}) collective-permute-start(f32[8,40,128]{2,1,0:T(8,128)S(1)} %constant_dynamic-slice_fusion), channel_id=1, source_target_pairs={{0,1},{1,0},{2,3},{3,2},{4,5},{5,4},{6,7},{7,6},{8,9},{9,8},{10,11... | collective-permute-start | bytes 491528 | tf_op jit(solution)/shard_map/ppermute | solution.py:318
  110.1 1.0 collective-permute-done.18
  111.1 3.8 %finish.1 = (f32[192,1536]{1,0:T(8,128)}, f32[6,8,384]{2,1,0:T(8,128)}) custom-call(s32[3]{0:T(128)S(1)} %copy-done.2, f32[1280,128]{1,0:T(8,128)S(1)} %bitcast.42, f32[320,128]{1,0:T(8,128)S(1)} %bitcast.55), custom_call_target="tpu_custom_call" | custom-call | flops 30000000 | bytes 1000000 | tf_op jit(solution)/shard_map/finish/pallas_call | solution.py:529
  (19 shorter events, 0.3 us)
Async XLA Ops:
  0.6 0.8 copy-start.1
  1.5 13.5 %copy-start = (f32[56,128]{1,0:T(8,128)}, f32[56,128]{1,0:T(8,128)S(1)}, u32[]{:S(2)}) copy-start(f32[56,128]{1,0:T(8,128)S(1)} %held.1.w_ref) | copy-start | bytes 86020
  1.5 5.3 %collective-permute-start.2 = (f32[56,128]{1,0:T(8,128)S(1)}, f32[56,128]{1,0:T(8,128)S(1)}, u32[]{:S(2)}, u32[]{:S(2)}) collective-permute-start(f32[56,128]{1,0:T(8,128)S(1)} %held.1.w_ref), channel_id=1, source_target_pairs={{0,66},{2,64},{64,2},{66,0},{1,67},{3,65},{65,3},{67,1},{4,70},{6,... | collective-permute-start | bytes 86024 | tf_op jit(solution)/shard_map/ppermute | solution.py:322
  4.9 2.8 %collective-permute-start.1 = (f32[56,128]{1,0:T(8,128)S(1)}, f32[56,128]{1,0:T(8,128)S(1)}, u32[]{:S(2)}, u32[]{:S(2)}) collective-permute-start(f32[56,128]{1,0:T(8,128)S(1)} %held.1.w_ref), channel_id=1, source_target_pairs={{0,64},{64,0},{1,65},{65,1},{2,66},{66,2},{3,67},{67,3},{4,68},{68... | collective-permute-start | bytes 86024 | tf_op jit(solution)/shard_map/ppermute | solution.py:318
  4.9 4.2 %collective-permute-start = (f32[56,128]{1,0:T(8,128)S(1)}, f32[56,128]{1,0:T(8,128)S(1)}, u32[]{:S(2)}, u32[]{:S(2)}) collective-permute-start(f32[56,128]{1,0:T(8,128)S(1)} %held.1.w_ref), channel_id=1, source_target_pairs={{0,2},{2,0},{1,3},{3,1},{4,6},{6,4},{5,7},{7,5},{8,10},{10,8},{9,1... | collective-permute-start | bytes 86024 | tf_op jit(solution)/shard_map/ppermute | solution.py:318
  9.2 12.4 %collective-permute-start.5 = (f32[2,112,128]{2,1,0:T(8,128)S(1)}, f32[2,112,128]{2,1,0:T(8,128)S(1)}, u32[]{:S(2)}, u32[]{:S(2)}) collective-permute-start(f32[2,112,128]{2,1,0:T(8,128)S(1)} %pad_maximum_fusion.1), channel_id=1, source_target_pairs={{0,16},{16,32},{32,48},{48,0},{1,17},{17,33},{33,49},{49,1},{2,18}... | collective-permute-start | bytes 344072 | tf_op jit(solution)/shard_map/ppermute | solution.py:314
  11.0 10.6 %collective-permute-start.4 = (f32[2,112,128]{2,1,0:T(8,128)S(1)}, f32[2,112,128]{2,1,0:T(8,128)S(1)}, u32[]{:S(2)}, u32[]{:S(2)}) collective-permute-start(f32[2,112,128]{2,1,0:T(8,128)S(1)} %pad_maximum_fusion.1), channel_id=1, source_target_pairs={{0,32},{16,48},{32,0},{48,16},{1,33},{17,49},{33,1},{49,17},{2,34}... | collective-permute-start | bytes 344072 | tf_op jit(solution)/shard_map/ppermute | solution.py:314
  14.3 7.3 %collective-permute-start.3 = (f32[2,112,128]{2,1,0:T(8,128)S(1)}, f32[2,112,128]{2,1,0:T(8,128)S(1)}, u32[]{:S(2)}, u32[]{:S(2)}) collective-permute-start(f32[2,112,128]{2,1,0:T(8,128)S(1)} %pad_maximum_fusion.1), channel_id=1, source_target_pairs={{0,48},{16,0},{32,16},{48,32},{1,49},{17,1},{33,17},{49,33},{2,50}... | collective-permute-start | bytes 344072 | tf_op jit(solution)/shard_map/ppermute | solution.py:314
  21.8 31.1 %all-to-all-start = ((f32[32,72,128]{2,1,0:T(8,128)}), f32[32,72,128]{2,1,0:T(8,128)S(1)}, u32[]{:S(2)}, u32[]{:S(2)}) async-start(f32[32,72,128]{2,1,0:T(8,128)} %bitcast.15), calls=%async_computation | async-start | bytes 2359296 | tf_op jit(solution)/shard_map/all_to_all | solution.py:548
  27.9 24.9 %collective-permute-start.11 = (f32[2,448,128]{2,1,0:T(8,128)S(1)}, f32[2,448,128]{2,1,0:T(8,128)S(1)}, u32[]{:S(2)}, u32[]{:S(2)}) collective-permute-start(f32[2,448,128]{2,1,0:T(8,128)S(1)} %bitcast.43), channel_id=1, source_target_pairs={{0,4},{4,8},{8,12},{12,0},{1,5},{5,9},{9,13},{13,1},{2,6},{6,10},{... | collective-permute-start | bytes 1376264 | tf_op jit(solution)/shard_map/ppermute | solution.py:314
  29.2 25.6 %collective-permute-start.10 = (f32[2,448,128]{2,1,0:T(8,128)S(1)}, f32[2,448,128]{2,1,0:T(8,128)S(1)}, u32[]{:S(2)}, u32[]{:S(2)}) collective-permute-start(f32[2,448,128]{2,1,0:T(8,128)S(1)} %bitcast.44), channel_id=1, source_target_pairs={{0,12},{4,0},{8,4},{12,8},{1,13},{5,1},{9,5},{13,9},{2,14},{6,2},{... | collective-permute-start | bytes 1376264 | tf_op jit(solution)/shard_map/ppermute | solution.py:314
  52.8 11.0 %copy-start.2 = (s32[3]{0:T(128)S(1)}, s32[3]{0:T(128)}, u32[]{:S(2)}) copy-start(s32[3]{0:T(128)} %pad_add_fusion.place_ref) | copy-start | bytes 40
  52.8 6.6 %collective-permute-start.12 = (f32[448,128]{1,0:T(8,128)S(1)}, f32[448,128]{1,0:T(8,128)S(1)}, u32[]{:S(2)}, u32[]{:S(2)}) collective-permute-start(f32[448,128]{1,0:T(8,128)S(1)} %slice_bitcast_fusion.1), channel_id=1, source_target_pairs={{0,4},{4,8},{8,12},{12,0},{1,5},{5,9},{9,13},{13,1},{2,6},{6,10},{... | collective-permute-start | bytes 688136 | tf_op jit(solution)/shard_map/ppermute | solution.py:314
  52.9 10.9 %collective-permute-start.6 = (f32[32,24,128]{2,1,0:T(8,128)S(1)}, f32[32,24,128]{2,1,0:T(8,128)S(1)}, u32[]{:S(2)}, u32[]{:S(2)}) collective-permute-start(f32[32,24,128]{2,1,0:T(8,128)S(1)} %slice.12), channel_id=1, source_target_pairs={{0,1},{1,0},{2,3},{3,2},{4,5},{5,4},{6,7},{7,6},{8,9},{9,8},{10,11... | collective-permute-start | bytes 1179656 | tf_op jit(solution)/shard_map/ppermute | solution.py:318
  54.9 7.9 %collective-permute-start.13 = (f32[448,128]{1,0:T(8,128)S(1)}, f32[448,128]{1,0:T(8,128)S(1)}, u32[]{:S(2)}, u32[]{:S(2)}) collective-permute-start(f32[448,128]{1,0:T(8,128)S(1)} %slice_bitcast_fusion), channel_id=1, source_target_pairs={{0,12},{4,0},{8,4},{12,8},{1,13},{5,1},{9,5},{13,9},{2,14},{6,2},{... | collective-permute-start | bytes 688136 | tf_op jit(solution)/shard_map/ppermute | solution.py:314
  57.9 16.8 %collective-permute-start.14 = (f32[896,128]{1,0:T(8,128)S(1)}, f32[896,128]{1,0:T(8,128)S(1)}, u32[]{:S(2)}, u32[]{:S(2)}) collective-permute-start(f32[896,128]{1,0:T(8,128)S(1)} %bitcast.45), channel_id=1, source_target_pairs={{0,1},{1,0},{2,3},{3,2},{4,5},{5,4},{6,7},{7,6},{8,9},{9,8},{10,11... | collective-permute-start | bytes 1376264 | tf_op jit(solution)/shard_map/ppermute | solution.py:318
  58.2 16.5 %collective-permute-start.17 = (f32[896,128]{1,0:T(8,128)S(1)}, f32[896,128]{1,0:T(8,128)S(1)}, u32[]{:S(2)}, u32[]{:S(2)}) collective-permute-start(f32[896,128]{1,0:T(8,128)S(1)} %bitcast.49), channel_id=1, source_target_pairs={{0,1},{1,0},{2,3},{3,2},{4,5},{5,4},{6,7},{7,6},{8,9},{9,8},{10,11... | collective-permute-start | bytes 1376264 | tf_op jit(solution)/shard_map/ppermute | solution.py:318
  59.4 15.3 %collective-permute-start.15 = (f32[896,128]{1,0:T(8,128)S(1)}, f32[896,128]{1,0:T(8,128)S(1)}, u32[]{:S(2)}, u32[]{:S(2)}) collective-permute-start(f32[896,128]{1,0:T(8,128)S(1)} %bitcast.51), channel_id=1, source_target_pairs={{0,1},{1,0},{2,3},{3,2},{4,5},{5,4},{6,7},{7,6},{8,9},{9,8},{10,11... | collective-permute-start | bytes 1376264 | tf_op jit(solution)/shard_map/ppermute | solution.py:318
  62.8 11.8 %collective-permute-start.16 = (f32[896,128]{1,0:T(8,128)S(1)}, f32[896,128]{1,0:T(8,128)S(1)}, u32[]{:S(2)}, u32[]{:S(2)}) collective-permute-start(f32[896,128]{1,0:T(8,128)S(1)} %bitcast.47), channel_id=1, source_target_pairs={{0,1},{1,0},{2,3},{3,2},{4,5},{5,4},{6,7},{7,6},{8,9},{9,8},{10,11... | collective-permute-start | bytes 1376264 | tf_op jit(solution)/shard_map/ppermute | solution.py:318
  65.2 1.5 %collective-permute-start.7 = (f32[288,128]{1,0:T(8,128)S(1)}, f32[288,128]{1,0:T(8,128)S(1)}, u32[]{:S(2)}, u32[]{:S(2)}) collective-permute-start(f32[288,128]{1,0:T(8,128)S(1)} %get-tuple-element.15), channel_id=1, source_target_pairs={{0,1},{1,0},{2,3},{3,2},{4,5},{5,4},{6,7},{7,6},{8,9},{9,8},{10,11... | collective-permute-start | bytes 442376 | tf_op jit(solution)/shard_map/ppermute | solution.py:318
  66.7 6.8 %collective-permute-start.8 = (f32[288,128]{1,0:T(8,128)S(1)}, f32[288,128]{1,0:T(8,128)S(1)}, u32[]{:S(2)}, u32[]{:S(2)}) collective-permute-start(f32[288,128]{1,0:T(8,128)S(1)} %add.20), channel_id=1, source_target_pairs={{0,2},{2,0},{1,3},{3,1},{4,6},{6,4},{5,7},{7,5},{8,10},{10,8},{9,1... | collective-permute-start | bytes 442376 | tf_op jit(solution)/shard_map/ppermute | solution.py:318
  73.6 2.8 %collective-permute-start.9 = (f32[288,128]{1,0:T(8,128)S(1)}, f32[288,128]{1,0:T(8,128)S(1)}, u32[]{:S(2)}, u32[]{:S(2)}) collective-permute-start(f32[288,128]{1,0:T(8,128)S(1)} %add.21.mine_ref), channel_id=1, source_target_pairs={{0,1},{1,0},{2,3},{3,2},{4,5},{5,4},{6,7},{7,6},{8,9},{9,8},{10,11... | collective-permute-start | bytes 442376 | tf_op jit(solution)/shard_map/ppermute | solution.py:318
  88.4 20.4 %all-to-all-start.1 = ((f32[32,40,128]{2,1,0:T(8,128)}), f32[32,40,128]{2,1,0:T(8,128)S(1)}, u32[]{:S(2)}, u32[]{:S(2)}) async-start(f32[32,40,128]{2,1,0:T(8,128)} %bitcast.26), calls=%async_computation.1 | async-start | bytes 1310720 | tf_op jit(solution)/shard_map/all_to_all | solution.py:548
  108.7 2.4 %collective-permute-start.18 = (f32[8,40,128]{2,1,0:T(8,128)S(1)}, f32[8,40,128]{2,1,0:T(8,128)S(1)}, u32[]{:S(2)}, u32[]{:S(2)}) collective-permute-start(f32[8,40,128]{2,1,0:T(8,128)S(1)} %constant_dynamic-slice_fusion), channel_id=1, source_target_pairs={{0,1},{1,0},{2,3},{3,2},{4,5},{5,4},{6,7},{7,6},{8,9},{9,8},{10,11... | collective-permute-start | bytes 491528 | tf_op jit(solution)/shard_map/ppermute | solution.py:318
